TPU v7x, 32 devices: a whole 2x2x4 slice. The times are simulated.
32 devices in a mesh: dp: 8 (over z, x), tensor: 4 (over y, core).
Axes of the slice: x: 2, y: 2, z: 4, core: 2. Of those that a mesh axis runs over, the one named last changes fastest.
Arguments:
- hidden_in: bfloat16 [32, 128, 4096], P(('dp', 'tensor')), parts along dimension 0, may hold values from -6 to 6
- norm_gain: float32 [4096], replicated, may hold values from 0.1 to 1.9
- query_weight: bfloat16 [4096, 4096], P(None, 'tensor'), may hold values from -3 to 3
- kv_weight: bfloat16 [4096, 2048], P(None, 'tensor'), may hold values from -3 to 3
- output_weight: bfloat16 [4096, 4096], P('tensor'), may hold values from -0.09375 to 0.09375
Outputs:
- attention_out: bfloat16 [32, 128, 4096], P(('dp', 'tensor')), parts along dimension 0
There are 8 independent parts, one for each index of `dp`. A program takes and returns all parts, laid end to end along the dimension named above; an argument that names none is the same for every part. Nothing has to cross between parts.
All inputs are finite; a program needn't handle non-finite values.
Results may differ from a plain program's by a relative error of at most 0.014.
The roundings to bfloat16 on the way count: a program that leaves them out, or rounds other values in their place, can miss the bound.
Values may be sent and summed in bfloat16 or wider, within the bound.
No kernel may reach another device: no remote copies, remote signals or barrier semaphores. Data moves between devices by JAX's collectives and lax.ppermute only.
A program may use at most 128 MiB of HBM per device.

v0:
```python
import math

import jax
import jax.numpy as jnp
from jax import lax
from jax.sharding import PartitionSpec as P

KVH = 8
HD = 128


EPS = 1e-05
THETA = 500000.0


def partner_2(value, axis, bit):
    mask = 2**bit
    pairs = [(source, source ^ mask) for source in range(lax.axis_size(axis))]
    return lax.ppermute(value, axis, pairs)


def rotary(tensor, positions):
    half_width = tensor.shape[-1] // 2
    frequency = THETA ** (-(jnp.arange(half_width, dtype=jnp.float32) * 2.0 / tensor.shape[-1]))
    angles = positions[:, None] * frequency[None, :]
    cosine = jnp.cos(angles)[:, None, :]
    sine_part = jnp.sin(angles)[:, None, :]
    first_half = tensor[..., :half_width]
    second_half = tensor[..., half_width:]
    return jnp.concatenate(
        (
            first_half * cosine - second_half * sine_part,
            second_half * cosine + first_half * sine_part,
        ),
        axis=-1,
    )


def rms_norm(hidden_in, norm_gain):
    wide = hidden_in.astype(jnp.float32)
    mean_square = jnp.mean(wide * wide, axis=-1, keepdims=True)
    return (wide * lax.rsqrt(mean_square + EPS) * norm_gain).astype(jnp.bfloat16)


def attend(queries, keys, values):
    length = queries.shape[1]
    scores = jnp.einsum(
        "bqhgd,bkhd->bhgqk", queries, keys, preferred_element_type=jnp.float32
    ) / math.sqrt(queries.shape[-1])
    causal = jnp.arange(length)[:, None] >= jnp.arange(length)[None, :]
    scores = jnp.where(causal, scores, -1e30)
    highest = jnp.max(scores, axis=-1, keepdims=True)
    exponent = jnp.exp(scores - highest)
    probabilities = (exponent / jnp.sum(exponent, axis=-1, keepdims=True)).astype(jnp.bfloat16)
    mixed = jnp.einsum(
        "bhgqk,bkhd->bqhgd", probabilities, values, preferred_element_type=jnp.float32
    )
    return mixed.astype(jnp.bfloat16)


def join_heads(stacked, axis_dim):
    sharers = max(lax.axis_size("tensor") // KVH, 1)
    position = lax.axis_index("tensor")
    for bit_index in range(sharers.bit_length() - 1):
        partner = partner_2(stacked, "tensor", bit_index)
        keeps_first = position // (1 << bit_index) % 2 == 0
        stacked = jnp.where(
            keeps_first,
            jnp.concatenate((stacked, partner), axis_dim),
            jnp.concatenate((partner, stacked), axis_dim),
        )
    return stacked


def shards(hidden_in, norm_gain, query_weight, kv_weight, output_weight):
    merged_weight = jnp.concatenate((query_weight, kv_weight), axis=1)
    query_cols = query_weight.shape[1]
    normed = rms_norm(hidden_in, norm_gain)
    projected = jnp.einsum(
        "brd,dc->brc",
        lax.all_gather(normed, "tensor", axis=0, tiled=True),
        merged_weight,
        preferred_element_type=jnp.float32,
    )
    batch, length = (projected.shape[0], projected.shape[1])
    queries_raw = projected[..., :query_cols]
    kv_raw = projected[..., query_cols:].astype(jnp.bfloat16)
    kv_raw = join_heads(kv_raw, 2)
    kv_heads = kv_raw.shape[-1] // (2 * HD)
    kv_split = kv_raw.reshape(batch, length, kv_heads, 2, HD)
    keys_raw = kv_split[:, :, :, 0, :]
    values = kv_split[:, :, :, 1, :]
    heads = query_cols // HD
    positions = jnp.arange(length, dtype=jnp.float32)
    queries = rotary(queries_raw.reshape(batch, length, heads, HD), positions).astype(jnp.bfloat16)
    keys = rotary(keys_raw.astype(jnp.float32), positions).astype(jnp.bfloat16)
    mixed = attend(queries.reshape(batch, length, kv_heads, heads // kv_heads, HD), keys, values)
    mixed_rows = mixed.reshape(batch, length, heads * HD)
    partial_out = jnp.einsum(
        "blc,cd->bld", mixed_rows, output_weight, preferred_element_type=jnp.float32
    )
    return lax.psum_scatter(
        partial_out.astype(jnp.bfloat16), "tensor", scatter_dimension=0, tiled=True
    )


def solution(mesh):
    placed = (
        P(("dp", "tensor"), None, None),
        P(),
        P(None, "tensor"),
        P(None, "tensor"),
        P("tensor", None),
    )
    return jax.shard_map(
        shards,
        mesh=mesh,
        in_specs=placed,
        out_specs=P(("dp", "tensor"), None, None),
        check_vma=False,
    )
```

profile of v0, /device:TPU:0, one launch (start us, length us, event | category | flops | bytes accessed | tf_op | source)
XLA Modules:
  0.0 133.2 jit_solution(11468829457427591245)
XLA Ops:
  6.5 0.0 all-gather.2.cloned.1.call-start
  6.5 1.5 %fusion.9 = f32[128]{0:T(128)S(1)} fusion(bf16[1,128,4096]{2,1,0:T(8,128)(2,1)} %param.5), kind=kLoop, calls=%fused_computation.10 | loop fusion | flops 1572736 | bytes 1049088 | tf_op jit(solution)/shard_map/reduce_sum | solution.py:41
  8.1 2.5 %fusion.11 = bf16[1,128,4096]{2,1,0:T(8,128)(2,1)} fusion(bf16[1,128,4096]{2,1,0:T(8,128)(2,1)} %param.5, f32[4096]{0:T(1024)} %param.6, f32[128]{0:T(128)S(1)} %add_rsqrt_fusion), kind=kLoop, calls=%fused_computation.12 | loop fusion | flops 2097152 | bytes 2114048 | tf_op jit(solution)/shard_map/convert_element_type | solution.py:42
  10.6 0.0 all-gather.2.cloned.1.call-update
  10.6 0.0 reduce-scatter.2.cloned.1.call-start
  10.7 0.3 fusion.29
  11.0 37.0 %all-gather.2.cloned.1.call-done = bf16[4,128,4096]{2,1,0:T(8,128)(2,1)} async-done(((bf16[1,128,4096]{2,1,0:T(8,128)(2,1)}), bf16[4,128,4096]{2,1,0:T(8,128)(2,1)}) %all-gather.2.cloned.1.call-update) | async-done | bytes 4194320 | tf_op jit(solution)/shard_map/all_gather | solution.py:81
  48.0 11.0 %fusion.1 = f32[4,128,1536]{2,1,0:T(8,128)S(1)} fusion(bf16[4,128,4096]{2,1,0:T(8,128)(2,1)} %all-gather.2.cloned.1.call-done, bf16[4096,512]{1,0:T(8,128)(2,1)} %param.8, bf16[4096,1024]{1,0:T(8,128)(2,1)} %param.7), kind=kOutput, calls=%fused_computation.2 | convolution fusion | flops 6467616768 | bytes 19922944 | tf_op jit(solution)/shard_map/brd,dc->brc/dot_general | solution.py:79
  59.0 0.0 copy-start
  59.0 1.0 slice.50
  59.9 0.9 copy-done
  60.8 2.0 %reshape.80 = bf16[4,128,2,2,128]{4,3,2,1,0:T(2,128)(2,1)} reshape(bf16[4,128,512]{2,1,0:T(8,128)(2,1)} %slice.50) | data formatting | bytes 1048576 | tf_op jit(solution)/shard_map/reshape | solution.py:90
  62.8 0.0 slice-start
  62.8 2.3 %fusion.38 = (bf16[4,128,2,1,128]{4,3,2,1,0:T(2,128)(2,1)S(1)}, bf16[4,128,2,1,128]{4,3,2,1,0:T(2,128)(2,1)S(1)}) fusion(bf16[4,128,2,2,128]{4,3,2,1,0:T(2,128)(2,1)} %reshape.80), kind=kLoop, calls=%fused_computation.47 | loop fusion | bytes 1048576 | tf_op jit(solution)/shard_map/slice | solution.py:92
  65.1 0.0 slice-done
  65.1 0.5 copy.24
  65.6 0.3 subtract_convert_fusion.1
  65.8 0.7 subtract_convert_fusion
  66.6 0.2 copy.14
  66.8 0.2 copy.15
  67.1 0.4 copy.22
  67.4 2.6 %fusion.39 = (f32[4,2,4,128]{3,2,1,0:T(4,128)S(1)}, f32[4,2,4,128,128]{3,4,2,1,0:T(8,128)}) fusion(pred[128,128]{0,1:T(8,128)(4,1)S(1)} %iota_compare_fusion, bf16[4,128,2,4,64]{4,1,3,2,0:T(8,128)(2,1)S(1)} %bitcast.53, bf16[4,128,2,4,64]{4,1,3,2,0:T(8,128)(2,1)S(1)} %bitcast.52, bf16[4,128,2,64]{3,1,2,0:T(8,128)(2,1)S(1)} %get-tuple-element.8, ...), kind=kOutput, calls=%fused_computation.48 | convolution fusion | flops 138936448 | bytes 3440640 | tf_op jit(solution)/shard_map/sub | solution.py:53
  70.1 2.0 %convolution_convert_fusion = bf16[4,2,128,4,128]{4,2,3,1,0:T(8,128)(2,1)S(1)} fusion(f32[4,2,4,128,128]{3,4,2,1,0:T(8,128)} %get-tuple-element.14, f32[4,2,4,128]{3,2,1,0:T(4,128)S(1)} %get-tuple-element.13, bf16[4,128,2,1,128]{1,4,2,0,3:T(8,128)(2,1)S(1)} %copy.22), kind=kOutput, calls=%fused_computation.19 | convolution fusion | flops 135790592 | bytes 3424256 | tf_op jit(solution)/shard_map/bhgqk,bkhd->bqhgd/dot_general | solution.py:55
  72.1 9.5 %fusion.6 = bf16[4,128,4096]{2,1,0:T(8,128)(2,1)} fusion(bf16[4,128,1024]{1,2,0:T(8,128)(2,1)S(1)} %bitcast.54, bf16[1024,4096]{1,0:T(8,128)(2,1)} %param.9), kind=kOutput, calls=%fused_computation.7 | convolution fusion | flops 4297064448 | bytes 13631488 | tf_op jit(solution)/shard_map/blc,cd->bld/dot_general | solution.py:99
  81.6 0.0 reduce-scatter.2.cloned.1.call-update
  81.6 44.7 %reduce-scatter.2.cloned.1.call-done = bf16[1,128,4096]{2,1,0:T(8,128)(2,1)} async-done(((bf16[4,128,4096]{2,1,0:T(8,128)(2,1)}), bf16[1,128,4096]{2,1,0:T(8,128)(2,1)}) %reduce-scatter.2.cloned.1.call-update) | async-done | bytes 1048592 | tf_op jit(solution)/shard_map/reduce_scatter | solution.py:102
  (4 shorter events, 0.1 us)
Async XLA Ops:
  6.5 41.4 %all-gather.2.cloned.1.call-start = ((), (), s32[]{:S(2)}) async-start(), calls=%async_computation.1 | async-start | bytes 5242880 | tf_op jit(solution)/shard_map/all_gather | solution.py:81
  10.6 115.7 %reduce-scatter.2.cloned.1.call-start = ((), (), s32[]{:S(2)}) async-start(), calls=%async_computation.2 | async-start | bytes 5242880 | tf_op jit(solution)/shard_map/reduce_scatter | solution.py:102
  59.0 1.8 %copy-start = (f32[4,128,1536]{2,1,0:T(8,128)}, f32[4,128,1536]{2,1,0:T(8,128)S(1)}, u32[]{:S(2)}) copy-start(f32[4,128,1536]{2,1,0:T(8,128)S(1)} %fusion.1) | copy-start | bytes 9437188
  62.8 2.3 %slice-start = ((f32[4,128,1536]{2,1,0:T(8,128)}), f32[4,128,1024]{2,1,0:T(8,128)S(1)}, s32[]{:S(2)}) async-start(f32[4,128,1536]{2,1,0:T(8,128)} %copy-done), calls=%async_computation.3 | async-start | bytes 4194304 | tf_op jit(solution)/shard_map/slice | solution.py:86
Sparse Core Ops, SparseCore 0:
  10.7 37.1 all-gather.1
  81.7 44.5 reduce-scatter.1
where the time goes:
time: 133 us
  waiting for transfers between devices  81.7 us (61%)
  matrix products  25.1 us (19%)
  between operations  13.5 us (10%)
  local copies, waits for them, and re-layouts  7.37 us (6%)
  other arithmetic  5.38 us (4%)
    reduce_scatter x1, waiting for transfers between devices, shards(): lax.psum_scatter(partial_out.astype(jnp.bfloat16), 'tensor', scatter_dime...  44.7 us
    all_gather x1, waiting for transfers between devices, shards(): lax.all_gather(normed, 'tensor', axis=0, tiled=True)  37 us
    dot_general x1, matrix products, shards(): jnp.einsum('brd,dc->brc', lax.all_gather(normed, 'tensor', axis=0, tiled=...  11 us
    dot_general x1, matrix products, shards(): jnp.einsum('blc,cd->bld', mixed_rows, output_weight, preferred_element_ty...  9.5 us
  transfers between devices with their start and end apart: 2, of which 2 were waited for; matrix products, arithmetic and copies ran while one was open for 0% of the time, Pallas kernels for 0%

commit v1 on v0

v1 whole, which is shorter than its diff:
```python
import functools
import math

import jax
import jax.numpy as jnp
from jax import lax
from jax.experimental import pallas as pl
from jax.experimental.pallas import tpu as pltpu
from jax.sharding import PartitionSpec as P


KVH = 8
HD = 128

EPS = 1e-05
THETA = 500000.0

CHUNKS = 2
K_STEPS = 2
OUT_STEPS = 4


def hop(value, bit):
    pairs = [(source, source ^ bit) for source in range(lax.axis_size("tensor"))]
    return lax.ppermute(value, "tensor", pairs)


def rotary_tables(length):
    half_width = HD // 2
    frequency = THETA ** (-(jnp.arange(half_width, dtype=jnp.float32) * 2.0 / HD))
    angles = jnp.arange(length, dtype=jnp.float32)[:, None] * frequency[None, :]
    cosine = jnp.cos(angles)
    sine = jnp.sin(angles)
    return (
        jnp.concatenate((cosine, cosine), axis=1),
        jnp.concatenate((-sine, sine), axis=1),
    )


def block_kernel(*refs, pieces, has_past, first, k_steps, kv_heads, group):
    hidden = refs[:pieces]
    gain, wq, wkv, wo, cosine_ref, sine_ref = refs[pieces : pieces + 6]
    at = pieces + 6
    past = refs[at] if has_past else None
    at += has_past
    outs = refs[at : at + pieces]
    kv_out, normed, q_acc, kv_acc, mixed_all = refs[at + pieces :]
    step = pl.program_id(0)
    k_at = step % k_steps
    head = step // k_steps
    seqs, tokens, width = hidden[0].shape
    rows = seqs * tokens
    k_block = width // k_steps

    @pl.when(step == 0)
    def _():
        for piece, ref in enumerate(hidden):
            for seq in range(seqs):
                wide = ref[seq].astype(jnp.float32)
                mean_square = jnp.mean(wide * wide, axis=-1, keepdims=True)
                result = (wide * lax.rsqrt(mean_square + EPS) * gain[...]).astype(jnp.bfloat16)
                base = piece * rows + seq * tokens
                for k in range(k_steps):
                    normed[k, base : base + tokens, :] = result[:, k * k_block : (k + 1) * k_block]

    @pl.when(step < kv_heads * k_steps)
    def _():
        x = normed[k_at]
        q_part = jnp.dot(x, wq[...], preferred_element_type=jnp.float32)
        kv_part = jnp.dot(x, wkv[...], preferred_element_type=jnp.float32)

        @pl.when(k_at == 0)
        def _():
            q_acc[...] = q_part
            kv_acc[...] = kv_part

        @pl.when(k_at > 0)
        def _():
            q_acc[...] += q_part
            kv_acc[...] += kv_part

    @pl.when((step < kv_heads * k_steps) & (k_at == k_steps - 1))
    def _():
        cosine = cosine_ref[...]
        sine = sine_ref[...]

        def rotate(value):
            return (value * cosine + pltpu.roll(value, HD // 2, 1) * sine).astype(jnp.bfloat16)

        scale = 1.0 / math.sqrt(HD)
        total = first + tokens
        query_at = lax.broadcasted_iota(jnp.int32, (group * tokens, total), 0) % tokens + first
        key_at = lax.broadcasted_iota(jnp.int32, (group * tokens, total), 1)
        causal = query_at >= key_at
        for seq in range(pieces * seqs):
            span = slice(seq * tokens, (seq + 1) * tokens)
            queries = jnp.concatenate(
                [rotate(q_acc[span, h * HD : (h + 1) * HD]) for h in range(group)], axis=0
            )
            raw = kv_acc[span, :].astype(jnp.bfloat16)
            keys = rotate(raw[:, :HD].astype(jnp.float32))
            values = raw[:, HD:]
            kv_out[seq, :, :HD] = keys
            kv_out[seq, :, HD:] = values
            if has_past:
                keys = jnp.concatenate((past[seq, :, :HD], keys), axis=0)
                values = jnp.concatenate((past[seq, :, HD:], values), axis=0)
            scores = lax.dot_general(
                queries, keys, (((1,), (1,)), ((), ())), preferred_element_type=jnp.float32
            )
            scores = jnp.where(causal, scores * scale, -1e30)
            highest = jnp.max(scores, axis=-1, keepdims=True)
            exponent = jnp.exp(scores - highest)
            total_weight = jnp.sum(exponent, axis=-1, keepdims=True)
            probabilities = (exponent / total_weight).astype(jnp.bfloat16)
            mixed = jnp.dot(probabilities, values, preferred_element_type=jnp.float32)
            mixed = mixed.astype(jnp.bfloat16)
            for h in range(group):
                mixed_all[head, span, h * HD : (h + 1) * HD] = mixed[
                    h * tokens : (h + 1) * tokens, :
                ]

    @pl.when(step >= kv_heads * k_steps)
    def _():
        joined = jnp.concatenate([mixed_all[h] for h in range(kv_heads)], axis=1)
        out = jnp.dot(joined, wo[...], preferred_element_type=jnp.float32)
        for piece, ref in enumerate(outs):
            for seq in range(seqs):
                base = piece * rows + seq * tokens
                ref[seq] = out[base : base + tokens].astype(ref.dtype)


def block(hidden, weights, tables, past, first):
    gain, wq, wkv, wo = weights
    pieces = len(hidden)
    seqs, tokens, width = hidden[0].shape
    rows = pieces * seqs * tokens
    kv_heads = wkv.shape[1] // (2 * HD)
    group = wq.shape[1] // HD // kv_heads
    k_block = width // K_STEPS
    attend_steps = kv_heads * K_STEPS
    out_block = wo.shape[1] // OUT_STEPS
    cosine, sine = (table[first : first + tokens] for table in tables)

    def whole(shape):
        return pl.BlockSpec(shape, lambda s: (0,) * len(shape))

    def weight_at(s):
        held = jnp.minimum(s, attend_steps - 1)
        return held % K_STEPS, held // K_STEPS

    def out_at(s):
        return jnp.maximum(s - attend_steps, 0)

    in_specs = [whole((seqs, tokens, width)) for _ in hidden] + [
        whole((1, width)),
        pl.BlockSpec((k_block, group * HD), weight_at),
        pl.BlockSpec((k_block, 2 * HD), weight_at),
        pl.BlockSpec((wo.shape[0], out_block), lambda s: (0, out_at(s))),
        whole((tokens, HD)),
        whole((tokens, HD)),
    ]
    operands = [*hidden, gain, wq, wkv, wo, cosine, sine]
    if past is not None:
        in_specs.append(
            pl.BlockSpec((pieces * seqs, first, 2 * HD), lambda s: (0, 0, weight_at(s)[1]))
        )
        operands.append(past)
    kernel = functools.partial(
        block_kernel,
        pieces=pieces,
        has_past=past is not None,
        first=first,
        k_steps=K_STEPS,
        kv_heads=kv_heads,
        group=group,
    )
    flops = 2 * rows * width * (wq.shape[1] + wkv.shape[1] + wo.shape[0])
    result = pl.pallas_call(
        kernel,
        grid=(attend_steps + OUT_STEPS,),
        in_specs=in_specs,
        out_specs=[
            pl.BlockSpec((seqs, tokens, out_block), lambda s: (0, 0, out_at(s))) for _ in hidden
        ]
        + [pl.BlockSpec((pieces * seqs, tokens, 2 * HD), lambda s: (0, 0, weight_at(s)[1]))],
        out_shape=[
            jax.ShapeDtypeStruct(
                (seqs, tokens, wo.shape[1]), jnp.bfloat16 if piece % 2 else jnp.float32
            )
            for piece in range(pieces)
        ]
        + [jax.ShapeDtypeStruct((pieces * seqs, tokens, wkv.shape[1]), jnp.bfloat16)],
        scratch_shapes=[
            pltpu.VMEM((K_STEPS, rows, k_block), jnp.bfloat16),
            pltpu.VMEM((rows, group * HD), jnp.float32),
            pltpu.VMEM((rows, 2 * HD), jnp.float32),
            pltpu.VMEM((kv_heads, rows, group * HD), jnp.bfloat16),
        ],
        compiler_params=pltpu.CompilerParams(
            dimension_semantics=("arbitrary",), vmem_limit_bytes=44 * 2**20
        ),
        cost_estimate=pl.CostEstimate(
            flops=flops,
            transcendentals=0,
            bytes_accessed=2 * (wq.size + wkv.size + wo.size),
        ),
    )(*operands)
    return result[:-1], result[-1]


def finish_kernel(*refs):
    *addends, _, out = refs
    total = addends[0][...]
    for ref in addends[1:]:
        total = total + ref[...].astype(jnp.float32)
    out[...] = total.astype(jnp.bfloat16)


def finish(own, whole_came, came, previous, c, chunk):
    seqs, _, width = own.shape
    column = width // 2
    ranged = pl.BlockSpec((seqs, chunk, column), lambda i: (0, c, i))
    single = pl.BlockSpec((seqs, chunk, column), lambda i: (0, 0, i))
    addends = [own, *whole_came, *came]
    specs = [ranged] * (1 + len(whole_came)) + [single] * len(came)
    aliases = {}
    if previous is None:
        previous = jnp.zeros((8, 128), jnp.bfloat16)
    else:
        aliases = {len(addends): 0}
    return pl.pallas_call(
        finish_kernel,
        grid=(width // column,),
        in_specs=specs + [pl.BlockSpec(memory_space=pl.ANY)],
        out_specs=ranged,
        out_shape=jax.ShapeDtypeStruct(own.shape, jnp.bfloat16),
        input_output_aliases=aliases,
        compiler_params=pltpu.CompilerParams(
            dimension_semantics=("arbitrary",), vmem_limit_bytes=16 * 2**20
        ),
    )(*addends, previous)


def join_heads(kv_weight):
    sharers = max(lax.axis_size("tensor") // KVH, 1)
    position = lax.axis_index("tensor")
    for bit_index in range(sharers.bit_length() - 1):
        bit = 1 << bit_index
        partner = hop(kv_weight, bit)
        keeps_first = position // bit % 2 == 0
        kv_weight = jnp.concatenate(
            (
                jnp.where(keeps_first, kv_weight, partner),
                jnp.where(keeps_first, partner, kv_weight),
            ),
            axis=1,
        )
    return kv_weight


def layer(hidden_in, norm_gain, query_weight, kv_weight, output_weight):
    parts = lax.axis_size("tensor")
    _, length, width = hidden_in.shape
    tables = rotary_tables(length)
    weights = (norm_gain.reshape(1, width), query_weight, join_heads(kv_weight), output_weight)
    near = [m for m in range(parts) if m < 2]
    far = [m for m in range(parts) if m >= 2]
    groups = [far[i : i + 2] for i in range(0, len(far), 2)]
    chunk = length // CHUNKS
    spans = [slice(c * chunk, (c + 1) * chunk) for c in range(CHUNKS)]

    arrived = {0: hidden_in}
    if len(near) > 1:
        arrived[1] = hop(hidden_in, 1)
    far_arrived = []
    for span in spans:
        held = {0: hidden_in[:, span]}
        for m in far:
            low = m & -m
            if m ^ low == 1:
                held[1] = arrived[1][:, span]
            held[m] = hop(held[m ^ low], low)
        far_arrived.append(held)

    near_out, _ = block([arrived[m] for m in near], weights, tables, None, 0)
    own = near_out[0]
    near_came = []
    if len(near) > 1:
        near_came = [hop(near_out[1], 1)]

    pasts = [None for _ in groups]
    result = None
    for c in range(CHUNKS):
        totals = {}
        for g, group in enumerate(groups):
            out, kv = block(
                [far_arrived[c][m] for m in group], weights, tables, pasts[g], c * chunk
            )
            pasts[g] = kv if pasts[g] is None else jnp.concatenate((pasts[g], kv), axis=1)
            totals.update(zip(group, out))
        came = []
        for m in reversed(far):
            low = m & -m
            back = hop(totals[m].astype(jnp.bfloat16), low)
            if m ^ low:
                totals[m ^ low] = totals[m ^ low] + back.astype(jnp.float32)
            else:
                came.append(back)
        result = finish(own, near_came, came, result, c, chunk)
    return result


def solution(mesh):
    placed = (
        P(("dp", "tensor"), None, None),
        P(),
        P(None, "tensor"),
        P(None, "tensor"),
        P("tensor", None),
    )
    return jax.shard_map(
        layer,
        mesh=mesh,
        in_specs=placed,
        out_specs=P(("dp", "tensor"), None, None),
        check_vma=False,
    )
```

time: 133 us -> 101 us (0.76)
  Pallas kernels: 0 us -> 43.9 us
  waiting for transfers between devices: 81.7 us -> 45 us
  matrix products: 25.1 us -> 0 us
  between operations: 13.5 us -> 0.08 us
  starting transfers between devices: 0.04 us -> 6.38 us
  other arithmetic: 5.38 us -> 0.65 us
  local copies, waits for them, and re-layouts: 7.37 us -> 4.18 us
    ppermute x0 -> x10, waiting for transfers between devices: none -> 45 us  [hop(): return lax.ppermute(value, 'tensor', pairs)]
    reduce_scatter x1 -> x0, waiting for transfers between devices: 44.7 us -> none  [shards(): lax.psum_scatter(partial_out.astype(jnp.bfloat16), 'tensor', scatter_dime...]
    pallas_call x0 -> x5, Pallas kernels: none -> 43.9 us  [the longest x3 41.8 us: block(): pl.pallas_call(kernel, grid=(attend_steps + OUT_STEPS,), in_specs=in_spec...]
    all_gather x1 -> x0, waiting for transfers between devices: 37 us -> none  [shards(): lax.all_gather(normed, 'tensor', axis=0, tiled=True)]
    dot_general x3 -> x0, matrix products: 22.5 us -> none  [the longest x1 11 us: shards(): jnp.einsum('brd,dc->brc', lax.all_gather(normed, 'tensor', axis=0, tiled=...]
    ppermute x0 -> x10, starting transfers between devices: none -> 6.38 us  [hop(): return lax.ppermute(value, 'tensor', pairs)]
    sub x1 -> x0, matrix products: 2.61 us -> none  [attend(): exponent = jnp.exp(scores - highest)]
    convert_element_type x2, other arithmetic: 2.57 us -> 0.18 us  [layer(): back = hop(totals[m].astype(jnp.bfloat16), low)]
  transfers between devices with their start and end apart: 2 -> 10, of which waited for: 2 -> 4; matrix products, arithmetic and copies ran while one was open for 0% -> 1% of each run, Pallas kernels for 0% -> 43%
where the time goes in v1:
time: 101 us; the launch traced here: 100 us
  waiting for transfers between devices  45 us (45%)
  Pallas kernels  43.9 us (43%)
  starting transfers between devices  6.38 us (6%)
  local copies, waits for them, and re-layouts  4.18 us (4%)
    ppermute x10, waiting for transfers between devices, hop(): return lax.ppermute(value, 'tensor', pairs)  45 us
    pallas_call x3, Pallas kernels, block(): pl.pallas_call(kernel, grid=(attend_steps + OUT_STEPS,), in_specs=in_spec...  41.8 us
    ppermute x10, starting transfers between devices, hop(): return lax.ppermute(value, 'tensor', pairs)  6.38 us
    unnamed x8, local copies, waits for them, and re-layouts  2.91 us
    pallas_call x2, Pallas kernels, finish(): pl.pallas_call(finish_kernel, grid=(width // column,), in_specs=specs + [...  2.1 us
  transfers between devices with their start and end apart: 10, of which 4 were waited for; matrix products, arithmetic and copies ran while one was open for 1% of the time, Pallas kernels for 43%

profile of v1, /device:TPU:0, one launch (start us, length us, event | category | flops | bytes accessed | tf_op | source)
XLA Modules:
  0.0 100.1 jit_solution(11026280630094778872)
XLA Ops:
  0.0 1.3 %fusion.7 = (bf16[1,64,4096]{2,1,0:T(8,128)(2,1)S(1)}, bf16[1,64,4096]{2,1,0:T(8,128)(2,1)S(1)}) fusion(bf16[1,128,4096]{2,1,0:T(8,128)(2,1)} %refs_0_.1), kind=kLoop, calls=%fused_computation.21 | loop fusion | bytes 2097152 | tf_op jit(solution)/shard_map/slice | solution.py:278
  1.3 3.1 %collective-permute-start.4 = (bf16[1,64,4096]{2,1,0:T(8,128)(2,1)S(1)}, bf16[1,64,4096]{2,1,0:T(8,128)(2,1)S(1)}, u32[]{:S(2)}, u32[]{:S(2)}) collective-permute-start(bf16[1,64,4096]{2,1,0:T(8,128)(2,1)S(1)} %get-tuple-element.19), channel_id=1, source_target_pairs={{0,2},{1,3},{2,0},{3,1},{4,6},{5,7},{6,4},{7,5},{8,10},{9,11},{10,... | collective-permute-start | bytes 1572872 | tf_op jit(solution)/shard_map/ppermute | solution.py:25
  4.3 0.1 collective-permute-start.2
  4.4 0.0 collective-permute-start
  4.4 12.7 %collective-permute-done.4.refs_0_ = bf16[1,64,4096]{2,1,0:T(8,128)(2,1)S(1)} collective-permute-done((bf16[1,64,4096]{2,1,0:T(8,128)(2,1)S(1)}, bf16[1,64,4096]{2,1,0:T(8,128)(2,1)S(1)}, u32[]{:S(2)}, u32[]{:S(2)}) %collective-permute-start.4) | collective-permute-done | bytes 524320 | tf_op jit(solution)/shard_map/ppermute | solution.py:25
  17.1 0.0 collective-permute-start.5
  17.1 10.4 %collective-permute-done.2.refs_0_ = bf16[1,64,4096]{2,1,0:T(8,128)(2,1)S(1)} collective-permute-done((bf16[1,64,4096]{2,1,0:T(8,128)(2,1)S(1)}, bf16[1,64,4096]{2,1,0:T(8,128)(2,1)S(1)}, u32[]{:S(2)}, u32[]{:S(2)}) %collective-permute-start.2) | collective-permute-done | bytes 524320 | tf_op jit(solution)/shard_map/ppermute | solution.py:25
  27.5 0.0 collective-permute-start.3
  27.5 0.3 fusion.6
  27.8 0.1 fusion.3
  27.9 0.1 pad_maximum_fusion
  28.0 0.0 collective-permute-done.5.refs_1_
  28.0 0.0 copy-start
  28.0 2.2 %copy-done = bf16[4096,512]{1,0:T(8,128)(2,1)S(1)} copy-done((bf16[4096,512]{1,0:T(8,128)(2,1)S(1)}, bf16[4096,512]{1,0:T(8,128)(2,1)}, u32[]{:S(2)}) %copy-start) | copy-done | bytes 4194328
  30.2 0.0 copy-start.3
  30.2 0.7 copy-done.3
  30.9 12.5 %shard_map.56 = (f32[1,64,4096]{2,1,0:T(8,128)S(1)}, bf16[1,64,4096]{2,1,0:T(8,128)(2,1)S(1)}, bf16[2,64,512]{2,1,0:T(8,128)(2,1)S(1)}) custom-call(bf16[1,64,4096]{2,1,0:T(8,128)(2,1)S(1)} %collective-permute-done.4.refs_0_, bf16[1,64,4096]{2,1,0:T(8,128)(2,1)S(1)} %collective-permute-done.5.refs_1_, f32[1,4096]{1,0:T(1,128)S(1)} %bitcast.1, ...), custom_call_target="tpu_custom_call" | custom-call | flops 2684354560 | bytes 20971520 | tf_op jit(solution)/shard_map/pallas_call | solution.py:179
  43.4 0.6 collective-permute-start.8
  44.0 0.0 collective-permute-done.3.refs_1_
  44.0 0.0 copy-start.1
  44.0 0.0 copy-start.2
  44.0 13.3 %shard_map.57 = (f32[1,64,4096]{2,1,0:T(8,128)S(1)}, bf16[1,64,4096]{2,1,0:T(8,128)(2,1)S(1)}, bf16[2,64,512]{2,1,0:T(8,128)(2,1)}) custom-call(bf16[1,64,4096]{2,1,0:T(8,128)(2,1)S(1)} %collective-permute-done.2.refs_0_, bf16[1,64,4096]{2,1,0:T(8,128)(2,1)S(1)} %collective-permute-done.3.refs_1_, f32[1,4096]{1,0:T(1,128)S(1)} %bitcast.2, ...), custom_call_target="tpu_custom_call" | custom-call | flops 2684354560 | bytes 20971520 | tf_op jit(solution)/shard_map/pallas_call | solution.py:179
  57.3 0.1 collective-permute-start.6
  57.4 0.0 collective-permute-done.refs_1_
  57.4 0.0 copy-done.1
  57.4 0.0 copy-done.2
  57.4 16.0 %shard_map.55 = (f32[1,128,4096]{2,1,0:T(8,128)S(1)}, bf16[1,128,4096]{2,1,0:T(8,128)(2,1)S(1)}, bf16[2,128,512]{2,1,0:T(8,128)(2,1)}) custom-call(bf16[1,128,4096]{2,1,0:T(8,128)(2,1)S(1)} %copy-done.2, bf16[1,128,4096]{2,1,0:T(8,128)(2,1)S(1)} %collective-permute-done.refs_1_, f32[1,4096]{1,0:T(1,128)S(1)} %bitcast.3, bf16[4096,1024]{1,0:T(8,128)(2,1)} %refs_3_.5, ...), custom_call_target="tpu_custom_call" | custom-call | flops 5368709120 | bytes 20971520 | tf_op jit(solution)/shard_map/pallas_call | solution.py:179
  73.3 0.5 collective-permute-start.1
  73.8 0.0 collective-permute-done.8
  73.8 0.1 add_convert_fusion
  73.9 1.8 %collective-permute-start.9 = (bf16[1,64,4096]{2,1,0:T(8,128)(2,1)S(1)}, bf16[1,64,4096]{2,1,0:T(8,128)(2,1)S(1)}, u32[]{:S(2)}, u32[]{:S(2)}) collective-permute-start(bf16[1,64,4096]{2,1,0:T(8,128)(2,1)S(1)} %add_convert_fusion), channel_id=1, source_target_pairs={{0,2},{1,3},{2,0},{3,1},{4,6},{5,7},{6,4},{7,5},{8,10},{9,11},{10,... | collective-permute-start | bytes 1572872 | tf_op jit(solution)/shard_map/ppermute | solution.py:25
  75.7 0.0 collective-permute-done.6
  75.7 0.1 add_convert_fusion.1
  75.8 0.3 collective-permute-start.7
  76.2 12.6 %collective-permute-done.9.refs_2_ = bf16[1,64,4096]{2,1,0:T(8,128)(2,1)S(1)} collective-permute-done((bf16[1,64,4096]{2,1,0:T(8,128)(2,1)S(1)}, bf16[1,64,4096]{2,1,0:T(8,128)(2,1)S(1)}, u32[]{:S(2)}, u32[]{:S(2)}) %collective-permute-start.9) | collective-permute-done | bytes 524320 | tf_op jit(solution)/shard_map/ppermute | solution.py:25
  88.8 0.0 collective-permute-done.1.refs_1_
  88.8 1.1 %shard_map.58.refs_3_ = bf16[1,128,4096]{2,1,0:T(8,128)(2,1)} custom-call(f32[1,128,4096]{2,1,0:T(8,128)S(1)} %get-tuple-element.12.refs_0_, bf16[1,128,4096]{2,1,0:T(8,128)(2,1)S(1)} %collective-permute-done.1.refs_1_, bf16[1,64,4096]{2,1,0:T(8,128)(2,1)S(1)} %collective-permute-done.9.refs_2_, bf16[8,128]{1,0:T(8,128)(2,1)S(1)} %broadcast_in_dim.2.refs_3_), custom_call_target="tpu_custom_call" | custom-call | tf_op jit(solution)/shard_map/pallas_call | solution.py:232
  89.8 9.3 %collective-permute-done.7.refs_2_ = bf16[1,64,4096]{2,1,0:T(8,128)(2,1)S(1)} collective-permute-done((bf16[1,64,4096]{2,1,0:T(8,128)(2,1)S(1)}, bf16[1,64,4096]{2,1,0:T(8,128)(2,1)S(1)}, u32[]{:S(2)}, u32[]{:S(2)}) %collective-permute-start.7) | collective-permute-done | bytes 524320 | tf_op jit(solution)/shard_map/ppermute | solution.py:25
  99.1 1.0 %shard_map.59 = bf16[1,128,4096]{2,1,0:T(8,128)(2,1)} custom-call(f32[1,128,4096]{2,1,0:T(8,128)S(1)} %get-tuple-element.12.refs_0_, bf16[1,128,4096]{2,1,0:T(8,128)(2,1)S(1)} %collective-permute-done.1.refs_1_, bf16[1,64,4096]{2,1,0:T(8,128)(2,1)S(1)} %collective-permute-done.7.refs_2_, ...), custom_call_target="tpu_custom_call", output_to_operand_aliasing={{}: (3, {})} | custom-call | tf_op jit(solution)/shard_map/pallas_call | solution.py:232
  (2 shorter events, 0.0 us)
Async XLA Ops:
  1.3 15.8 %collective-permute-start.4 = (bf16[1,64,4096]{2,1,0:T(8,128)(2,1)S(1)}, bf16[1,64,4096]{2,1,0:T(8,128)(2,1)S(1)}, u32[]{:S(2)}, u32[]{:S(2)}) collective-permute-start(bf16[1,64,4096]{2,1,0:T(8,128)(2,1)S(1)} %get-tuple-element.19), channel_id=1, source_target_pairs={{0,2},{1,3},{2,0},{3,1},{4,6},{5,7},{6,4},{7,5},{8,10},{9,11},{10,... | collective-permute-start | bytes 1572872 | tf_op jit(solution)/shard_map/ppermute | solution.py:25
  4.3 23.2 %collective-permute-start.2 = (bf16[1,64,4096]{2,1,0:T(8,128)(2,1)S(1)}, bf16[1,64,4096]{2,1,0:T(8,128)(2,1)S(1)}, u32[]{:S(2)}, u32[]{:S(2)}) collective-permute-start(bf16[1,64,4096]{2,1,0:T(8,128)(2,1)S(1)} %get-tuple-element.20), channel_id=1, source_target_pairs={{0,2},{1,3},{2,0},{3,1},{4,6},{5,7},{6,4},{7,5},{8,10},{9,11},{10,... | collective-permute-start | bytes 1572872 | tf_op jit(solution)/shard_map/ppermute | solution.py:25
  4.4 53.0 %collective-permute-start = (bf16[1,128,4096]{2,1,0:T(8,128)(2,1)}, bf16[1,128,4096]{2,1,0:T(8,128)(2,1)S(1)}, u32[]{:S(2)}, u32[]{:S(2)}) collective-permute-start(bf16[1,128,4096]{2,1,0:T(8,128)(2,1)} %refs_0_.1), channel_id=1, source_target_pairs={{0,1},{1,0},{2,3},{3,2},{4,5},{5,4},{6,7},{7,6},{8,9},{9,8},{10,11... | collective-permute-start | bytes 3145736 | tf_op jit(solution)/shard_map/ppermute | solution.py:25
  17.1 10.9 %collective-permute-start.5 = (bf16[1,64,4096]{2,1,0:T(8,128)(2,1)S(1)}, bf16[1,64,4096]{2,1,0:T(8,128)(2,1)S(1)}, u32[]{:S(2)}, u32[]{:S(2)}) collective-permute-start(bf16[1,64,4096]{2,1,0:T(8,128)(2,1)S(1)} %collective-permute-done.4.refs_0_), channel_id=1, source_target_pairs={{0,1},{1,0},{2,3},{3,2},{4,5},{5,4},{6,7},{7,6},{8,9},{9,8},{10,11... | collective-permute-start | bytes 1572872 | tf_op jit(solution)/shard_map/ppermute | solution.py:25
  27.5 16.5 %collective-permute-start.3 = (bf16[1,64,4096]{2,1,0:T(8,128)(2,1)S(1)}, bf16[1,64,4096]{2,1,0:T(8,128)(2,1)S(1)}, u32[]{:S(2)}, u32[]{:S(2)}) collective-permute-start(bf16[1,64,4096]{2,1,0:T(8,128)(2,1)S(1)} %collective-permute-done.2.refs_0_), channel_id=1, source_target_pairs={{0,1},{1,0},{2,3},{3,2},{4,5},{5,4},{6,7},{7,6},{8,9},{9,8},{10,11... | collective-permute-start | bytes 1572872 | tf_op jit(solution)/shard_map/ppermute | solution.py:25
  28.0 2.2 %copy-start = (bf16[4096,512]{1,0:T(8,128)(2,1)S(1)}, bf16[4096,512]{1,0:T(8,128)(2,1)}, u32[]{:S(2)}) copy-start(bf16[4096,512]{1,0:T(8,128)(2,1)} %refs_4_.5) | copy-start | bytes 12582916
  30.2 0.7 copy-start.3
  43.4 30.4 %collective-permute-start.8 = (bf16[1,64,4096]{2,1,0:T(8,128)(2,1)S(1)}, bf16[1,64,4096]{2,1,0:T(8,128)(2,1)S(1)}, u32[]{:S(2)}, u32[]{:S(2)}) collective-permute-start(bf16[1,64,4096]{2,1,0:T(8,128)(2,1)S(1)} %get-tuple-element.18), channel_id=1, source_target_pairs={{0,1},{1,0},{2,3},{3,2},{4,5},{5,4},{6,7},{7,6},{8,9},{9,8},{10,11... | collective-permute-start | bytes 1572872 | tf_op jit(solution)/shard_map/ppermute | solution.py:25
  44.0 13.4 %copy-start.1 = (bf16[4096,512]{1,0:T(8,128)(2,1)S(1)}, bf16[4096,512]{1,0:T(8,128)(2,1)}, u32[]{:S(2)}) copy-start(bf16[4096,512]{1,0:T(8,128)(2,1)} %refs_4_.5) | copy-start | bytes 12582916
  44.0 13.4 %copy-start.2 = (bf16[1,128,4096]{2,1,0:T(8,128)(2,1)S(1)}, bf16[1,128,4096]{2,1,0:T(8,128)(2,1)}, u32[]{:S(2)}) copy-start(bf16[1,128,4096]{2,1,0:T(8,128)(2,1)} %refs_0_.1) | copy-start | bytes 3145732
  57.3 18.4 %collective-permute-start.6 = (bf16[1,64,4096]{2,1,0:T(8,128)(2,1)S(1)}, bf16[1,64,4096]{2,1,0:T(8,128)(2,1)S(1)}, u32[]{:S(2)}, u32[]{:S(2)}) collective-permute-start(bf16[1,64,4096]{2,1,0:T(8,128)(2,1)S(1)} %get-tuple-element.16), channel_id=1, source_target_pairs={{0,1},{1,0},{2,3},{3,2},{4,5},{5,4},{6,7},{7,6},{8,9},{9,8},{10,11... | collective-permute-start | bytes 1572872 | tf_op jit(solution)/shard_map/ppermute | solution.py:25
  73.3 15.4 %collective-permute-start.1 = (bf16[1,128,4096]{2,1,0:T(8,128)(2,1)S(1)}, bf16[1,128,4096]{2,1,0:T(8,128)(2,1)S(1)}, u32[]{:S(2)}, u32[]{:S(2)}) collective-permute-start(bf16[1,128,4096]{2,1,0:T(8,128)(2,1)S(1)} %get-tuple-element.13), channel_id=1, source_target_pairs={{0,1},{1,0},{2,3},{3,2},{4,5},{5,4},{6,7},{7,6},{8,9},{9,8},{10,11... | collective-permute-start | bytes 3145736 | tf_op jit(solution)/shard_map/ppermute | solution.py:25
  73.9 14.9 %collective-permute-start.9 = (bf16[1,64,4096]{2,1,0:T(8,128)(2,1)S(1)}, bf16[1,64,4096]{2,1,0:T(8,128)(2,1)S(1)}, u32[]{:S(2)}, u32[]{:S(2)}) collective-permute-start(bf16[1,64,4096]{2,1,0:T(8,128)(2,1)S(1)} %add_convert_fusion), channel_id=1, source_target_pairs={{0,2},{1,3},{2,0},{3,1},{4,6},{5,7},{6,4},{7,5},{8,10},{9,11},{10,... | collective-permute-start | bytes 1572872 | tf_op jit(solution)/shard_map/ppermute | solution.py:25
  75.8 23.3 %collective-permute-start.7 = (bf16[1,64,4096]{2,1,0:T(8,128)(2,1)S(1)}, bf16[1,64,4096]{2,1,0:T(8,128)(2,1)S(1)}, u32[]{:S(2)}, u32[]{:S(2)}) collective-permute-start(bf16[1,64,4096]{2,1,0:T(8,128)(2,1)S(1)} %add_convert_fusion.1), channel_id=1, source_target_pairs={{0,2},{1,3},{2,0},{3,1},{4,6},{5,7},{6,4},{7,5},{8,10},{9,11},{10,... | collective-permute-start | bytes 1572872 | tf_op jit(solution)/shard_map/ppermute | solution.py:25

commit v2 on v1

v2 whole, which is shorter than its diff:
```python
import functools
import math

import jax
import jax.numpy as jnp
from jax import lax
from jax.experimental import pallas as pl
from jax.experimental.pallas import tpu as pltpu
from jax.sharding import PartitionSpec as P


KVH = 8
HD = 128

EPS = 1e-05
THETA = 500000.0

CHUNKS = 2
K_STEPS = 2
OUT_STEPS = 4
VMEM_LIMIT = 12 * 2**20


def hop(value, bit):
    pairs = [(source, source ^ bit) for source in range(lax.axis_size("tensor"))]
    return lax.ppermute(value, "tensor", pairs)


def rotary_tables(length):
    half_width = HD // 2
    frequency = THETA ** (-(jnp.arange(half_width, dtype=jnp.float32) * 2.0 / HD))
    angles = jnp.arange(length, dtype=jnp.float32)[:, None] * frequency[None, :]
    cosine = jnp.cos(angles)
    sine = jnp.sin(angles)
    return (
        jnp.concatenate((cosine, cosine), axis=1),
        jnp.concatenate((-sine, sine), axis=1),
    )


def block_kernel(*refs, pieces, load, has_past, first, kv_heads, group):
    hidden = list(refs[:pieces])
    gain, wq, wkv, wo, cosine_ref, sine_ref = refs[pieces : pieces + 6]
    at = pieces + 6
    past = refs[at] if has_past else None
    at += has_past
    outs = refs[at : at + pieces]
    at += pieces
    copies = {}
    if load:
        wq_to, wkv_to, wo_to, normed, q_acc, kv_acc, mixed_all, held, gain_to, sems = refs[at:]
        k_steps = K_STEPS
    else:
        kv_out, normed, q_acc, kv_acc, mixed_all = refs[at:]
        k_steps = 1
    seqs, tokens, width = hidden[0].shape
    rows = seqs * tokens
    k_block = width // k_steps
    out_block = wo.shape[1] // OUT_STEPS

    def k_span(k):
        return slice(k * k_block, (k + 1) * k_block)

    def q_span(head):
        return slice(head * group * HD, (head + 1) * group * HD)

    def kv_span(head):
        return slice(head * 2 * HD, (head + 1) * 2 * HD)

    def out_span(n):
        return slice(n * out_block, (n + 1) * out_block)

    if load:

        def start(name, source, target):
            copy = pltpu.make_async_copy(source, target, sems.at[len(copies)])
            copy.start()
            copies[name] = copy

        start("gain", gain, gain_to)
        for piece, ref in enumerate(hidden):
            start(("x", piece), ref, held.at[piece])
            hidden[piece] = held.at[piece]
        for head in range(kv_heads):
            for k in range(k_steps):
                source = (k_span(k), q_span(head))
                start(("q", head, k), wq.at[source], wq_to.at[source])
                source = (k_span(k), kv_span(head))
                start(("kv", head, k), wkv.at[source], wkv_to.at[source])
        for n in range(OUT_STEPS):
            source = (slice(None), out_span(n))
            start(("o", n), wo.at[source], wo_to.at[source])
        gain, wq, wkv, wo = gain_to, wq_to, wkv_to, wo_to

    def ready(*name):
        if load:
            copies[name if len(name) > 1 else name[0]].wait()

    ready("gain")
    for piece, ref in enumerate(hidden):
        ready("x", piece)
        for seq in range(seqs):
            wide = ref[seq].astype(jnp.float32)
            mean_square = jnp.mean(wide * wide, axis=-1, keepdims=True)
            result = (wide * lax.rsqrt(mean_square + EPS) * gain[...]).astype(jnp.bfloat16)
            base = piece * rows + seq * tokens
            normed[base : base + tokens, :] = result

    cosine = cosine_ref[...]
    sine = sine_ref[...]

    def rotate(value):
        return (value * cosine + pltpu.roll(value, HD // 2, 1) * sine).astype(jnp.bfloat16)

    scale = 1.0 / math.sqrt(HD)
    total = first + tokens
    query_at = lax.broadcasted_iota(jnp.int32, (tokens, total), 0) + first
    key_at = lax.broadcasted_iota(jnp.int32, (tokens, total), 1)
    causal = jnp.concatenate([query_at - key_at] * group, axis=0) >= 0

    for head in range(kv_heads):
        for k in range(k_steps):
            ready("q", head, k)
            ready("kv", head, k)
            x = normed[:, k_span(k)]
            q_part = jnp.dot(x, wq[k_span(k), q_span(head)], preferred_element_type=jnp.float32)
            kv_part = jnp.dot(x, wkv[k_span(k), kv_span(head)], preferred_element_type=jnp.float32)
            if k == 0:
                q_acc[head] = q_part
                kv_acc[head] = kv_part
            else:
                q_acc[head] += q_part
                kv_acc[head] += kv_part
        for seq in range(pieces * seqs):
            span = slice(seq * tokens, (seq + 1) * tokens)
            queries = jnp.concatenate(
                [rotate(q_acc[head, span, h * HD : (h + 1) * HD]) for h in range(group)], axis=0
            )
            raw = kv_acc[head, span, :].astype(jnp.bfloat16)
            keys = rotate(raw[:, :HD].astype(jnp.float32))
            values = raw[:, HD:]
            if not load:
                kv_out[seq, :, head * 2 * HD : (head * 2 + 1) * HD] = keys
                kv_out[seq, :, (head * 2 + 1) * HD : (head * 2 + 2) * HD] = values
            if has_past:
                before = past[seq, :, kv_span(head)]
                keys = jnp.concatenate((before[:, :HD], keys), axis=0)
                values = jnp.concatenate((before[:, HD:], values), axis=0)
            scores = lax.dot_general(
                queries, keys, (((1,), (1,)), ((), ())), preferred_element_type=jnp.float32
            )
            scores = jnp.where(causal, scores * scale, -1e30)
            highest = jnp.max(scores, axis=-1, keepdims=True)
            exponent = jnp.exp(scores - highest)
            total_weight = jnp.sum(exponent, axis=-1, keepdims=True)
            probabilities = (exponent / total_weight).astype(jnp.bfloat16)
            mixed = jnp.dot(probabilities, values, preferred_element_type=jnp.float32)
            mixed = mixed.astype(jnp.bfloat16)
            for h in range(group):
                column = (head * group + h) * HD
                mixed_all[span, column : column + HD] = mixed[h * tokens : (h + 1) * tokens, :]

    for n in range(OUT_STEPS):
        ready("o", n)
        out = jnp.dot(mixed_all[...], wo[:, out_span(n)], preferred_element_type=jnp.float32)
        for piece, ref in enumerate(outs):
            for seq in range(seqs):
                base = piece * rows + seq * tokens
                ref[seq, :, out_span(n)] = out[base : base + tokens].astype(ref.dtype)


def block(hidden, weights, tables, past, first, load):
    gain, wq, wkv, wo = weights
    pieces = len(hidden)
    seqs, tokens, width = hidden[0].shape
    rows = pieces * seqs * tokens
    kv_heads = wkv.shape[1] // (2 * HD)
    group = wq.shape[1] // HD // kv_heads
    cosine, sine = (table[first : first + tokens] for table in tables)
    vmem = pl.BlockSpec(memory_space=pltpu.VMEM)
    source = pl.BlockSpec(memory_space=pl.ANY) if load else vmem
    held = pltpu.HBM if load else pltpu.VMEM
    wq, wkv, wo = (pltpu.with_memory_space_constraint(w, held) for w in (wq, wkv, wo))
    if load:
        gain = pltpu.with_memory_space_constraint(gain, held)
        hidden = [pltpu.with_memory_space_constraint(hidden[0], held), *hidden[1:]]
    operands = [*hidden, gain, wq, wkv, wo, cosine, sine]
    in_specs = [source] * (pieces + 4) + [vmem, vmem]
    if load:
        for at in (0, *range(pieces, pieces + 4)):
            in_specs[at] = pl.BlockSpec(memory_space=pltpu.HBM)
    if past is not None:
        operands.append(past)
        in_specs.append(vmem)
    out_shape = [
        jax.ShapeDtypeStruct(
            (seqs, tokens, wo.shape[1]), jnp.bfloat16 if piece % 2 else jnp.float32
        )
        for piece in range(pieces)
    ]
    scratch = [
        pltpu.VMEM((rows, width), jnp.bfloat16),
        pltpu.VMEM((kv_heads, rows, group * HD), jnp.float32),
        pltpu.VMEM((kv_heads, rows, 2 * HD), jnp.float32),
        pltpu.VMEM((rows, wq.shape[1]), jnp.bfloat16),
    ]
    if load:
        out_shape += [pltpu.VMEM(w.shape, w.dtype) for w in (wq, wkv, wo)]
        scratch += [
            pltpu.VMEM((pieces, seqs, tokens, width), hidden[0].dtype),
            pltpu.VMEM(gain.shape, gain.dtype),
            pltpu.SemaphoreType.DMA((1 + pieces + 2 * kv_heads * K_STEPS + OUT_STEPS,)),
        ]
    else:
        out_shape += [jax.ShapeDtypeStruct((pieces * seqs, tokens, wkv.shape[1]), jnp.bfloat16)]
    kernel = functools.partial(
        block_kernel,
        pieces=pieces,
        load=load,
        has_past=past is not None,
        first=first,
        kv_heads=kv_heads,
        group=group,
    )
    flops = 2 * rows * width * (wq.shape[1] + wkv.shape[1] + wo.shape[0])
    result = pl.pallas_call(
        kernel,
        in_specs=in_specs,
        out_specs=[vmem] * len(out_shape),
        out_shape=out_shape,
        scratch_shapes=scratch,
        compiler_params=pltpu.CompilerParams(vmem_limit_bytes=VMEM_LIMIT),
        cost_estimate=pl.CostEstimate(
            flops=flops,
            transcendentals=0,
            bytes_accessed=2 * (wq.size + wkv.size + wo.size),
        ),
    )(*operands)
    return result[:pieces], result[pieces:]


def finish_kernel(*refs):
    *addends, _, out = refs
    total = addends[0][...]
    for ref in addends[1:]:
        total = total + ref[...].astype(jnp.float32)
    out[...] = total.astype(jnp.bfloat16)


def finish(own, whole_came, came, previous, c, chunk):
    seqs, _, width = own.shape
    column = width // 2
    ranged = pl.BlockSpec((seqs, chunk, column), lambda i: (0, c, i))
    single = pl.BlockSpec((seqs, chunk, column), lambda i: (0, 0, i))
    addends = [own, *whole_came, *came]
    specs = [ranged] * (1 + len(whole_came)) + [single] * len(came)
    aliases = {}
    if previous is None:
        previous = jnp.zeros((8, 128), jnp.bfloat16)
    else:
        aliases = {len(addends): 0}
    return pl.pallas_call(
        finish_kernel,
        grid=(width // column,),
        in_specs=specs + [pl.BlockSpec(memory_space=pl.ANY)],
        out_specs=ranged,
        out_shape=jax.ShapeDtypeStruct(own.shape, jnp.bfloat16),
        input_output_aliases=aliases,
        compiler_params=pltpu.CompilerParams(
            dimension_semantics=("arbitrary",), vmem_limit_bytes=16 * 2**20
        ),
    )(*addends, previous)


def join_heads(kv_weight):
    sharers = max(lax.axis_size("tensor") // KVH, 1)
    position = lax.axis_index("tensor")
    for bit_index in range(sharers.bit_length() - 1):
        bit = 1 << bit_index
        partner = hop(kv_weight, bit)
        keeps_first = position // bit % 2 == 0
        kv_weight = jnp.concatenate(
            (
                jnp.where(keeps_first, kv_weight, partner),
                jnp.where(keeps_first, partner, kv_weight),
            ),
            axis=1,
        )
    return kv_weight


def layer(hidden_in, norm_gain, query_weight, kv_weight, output_weight):
    parts = lax.axis_size("tensor")
    _, length, width = hidden_in.shape
    tables = rotary_tables(length)
    weights = (norm_gain.reshape(1, width), query_weight, join_heads(kv_weight), output_weight)
    near = [m for m in range(parts) if m < 2]
    far = [m for m in range(parts) if m >= 2]
    groups = [far[i : i + 2] for i in range(0, len(far), 2)]
    chunk = length // CHUNKS
    spans = [slice(c * chunk, (c + 1) * chunk) for c in range(CHUNKS)]

    arrived = {0: hidden_in}
    if len(near) > 1:
        arrived[1] = hop(hidden_in, 1)
    far_arrived = []
    for span in spans:
        held = {0: hidden_in[:, span]}
        for m in far:
            low = m & -m
            if m ^ low == 1:
                held[1] = arrived[1][:, span]
            held[m] = hop(held[m ^ low], low)
        far_arrived.append(held)

    near_out, held_weights = block([arrived[m] for m in near], weights, tables, None, 0, True)
    weights = (weights[0], *held_weights)
    own = near_out[0]
    near_came = []
    if len(near) > 1:
        near_came = [hop(near_out[1], 1)]

    pasts = [None for _ in groups]
    result = None
    for c in range(CHUNKS):
        totals = {}
        for g, group in enumerate(groups):
            out, (kv,) = block(
                [far_arrived[c][m] for m in group], weights, tables, pasts[g], c * chunk, False
            )
            pasts[g] = kv if pasts[g] is None else jnp.concatenate((pasts[g], kv), axis=1)
            totals.update(zip(group, out))
        came = []
        for m in reversed(far):
            low = m & -m
            back = hop(totals[m].astype(jnp.bfloat16), low)
            if m ^ low:
                totals[m ^ low] = totals[m ^ low] + back.astype(jnp.float32)
            else:
                came.append(back)
        result = finish(own, near_came, came, result, c, chunk)
    return result


def solution(mesh):
    placed = (
        P(("dp", "tensor"), None, None),
        P(),
        P(None, "tensor"),
        P(None, "tensor"),
        P("tensor", None),
    )
    return jax.shard_map(
        layer,
        mesh=mesh,
        in_specs=placed,
        out_specs=P(("dp", "tensor"), None, None),
        check_vma=False,
    )
```

time: 101 us -> 79 us (0.78)
  Pallas kernels: 43.9 us -> 25.2 us
  local copies, waits for them, and re-layouts: 4.18 us -> 1.27 us
  starting transfers between devices: 6.38 us -> 7.53 us
    pallas_call x3, Pallas kernels: 41.8 us -> 23.1 us  [block(): pl.pallas_call(kernel, in_specs=in_specs, out_specs=[vmem] * len(out_shap...]
    unnamed x8 -> x2, local copies, waits for them, and re-layouts: 2.91 us -> 0.01 us
    ppermute x10, starting transfers between devices: 6.38 us -> 7.53 us  [hop(): return lax.ppermute(value, 'tensor', pairs)]
  transfers between devices with their start and end apart: 10 -> 10, of which waited for: 4 -> 4; matrix products, arithmetic and copies ran while one was open for 1% -> 2% of each run, Pallas kernels for 43% -> 31%
where the time goes in v2:
time: 79 us; the launch traced here: 78.9 us
  waiting for transfers between devices  44.1 us (56%)
  Pallas kernels  25.2 us (32%)
  starting transfers between devices  7.53 us (10%)
  local copies, waits for them, and re-layouts  1.27 us (2%)
    ppermute x10, waiting for transfers between devices, hop(): return lax.ppermute(value, 'tensor', pairs)  44.1 us
    pallas_call x3, Pallas kernels, block(): pl.pallas_call(kernel, in_specs=in_specs, out_specs=[vmem] * len(out_shap...  23.1 us
    ppermute x10, starting transfers between devices, hop(): return lax.ppermute(value, 'tensor', pairs)  7.53 us
    pallas_call x2, Pallas kernels, finish(): pl.pallas_call(finish_kernel, grid=(width // column,), in_specs=specs + [...  2.1 us
  transfers between devices with their start and end apart: 10, of which 4 were waited for; matrix products, arithmetic and copies ran while one was open for 2% of the time, Pallas kernels for 31%

profile of v2, /device:TPU:0, one launch (start us, length us, event | category | flops | bytes accessed | tf_op | source)
XLA Modules:
  0.0 78.9 jit_solution(13273406445789813440)
XLA Ops:
  0.0 0.5 collective-permute-start
  0.5 1.3 %fusion.7 = (bf16[1,64,4096]{2,1,0:T(8,128)(2,1)S(1)}, bf16[1,64,4096]{2,1,0:T(8,128)(2,1)S(1)}) fusion(bf16[1,128,4096]{2,1,0:T(8,128)(2,1)} %refs_0_.1), kind=kLoop, calls=%fused_computation.21 | loop fusion | bytes 2097152 | tf_op jit(solution)/shard_map/slice | solution.py:308
  1.8 2.6 %collective-permute-start.4 = (bf16[1,64,4096]{2,1,0:T(8,128)(2,1)S(1)}, bf16[1,64,4096]{2,1,0:T(8,128)(2,1)S(1)}, u32[]{:S(2)}, u32[]{:S(2)}) collective-permute-start(bf16[1,64,4096]{2,1,0:T(8,128)(2,1)S(1)} %get-tuple-element.25), channel_id=1, source_target_pairs={{0,2},{1,3},{2,0},{3,1},{4,6},{5,7},{6,4},{7,5},{8,10},{9,11},{10,... | collective-permute-start | bytes 1572872 | tf_op jit(solution)/shard_map/ppermute | solution.py:26
  4.3 0.1 collective-permute-start.2
  4.4 0.3 fusion.6
  4.7 0.1 pad_maximum_fusion
  4.8 12.3 %collective-permute-done.4.refs_0_ = bf16[1,64,4096]{2,1,0:T(8,128)(2,1)S(1)} collective-permute-done((bf16[1,64,4096]{2,1,0:T(8,128)(2,1)S(1)}, bf16[1,64,4096]{2,1,0:T(8,128)(2,1)S(1)}, u32[]{:S(2)}, u32[]{:S(2)}) %collective-permute-start.4) | collective-permute-done | bytes 524320 | tf_op jit(solution)/shard_map/ppermute | solution.py:26
  17.1 0.0 collective-permute-start.5
  17.1 0.1 fusion.3
  17.2 10.9 %collective-permute-done.2.refs_0_ = bf16[1,64,4096]{2,1,0:T(8,128)(2,1)S(1)} collective-permute-done((bf16[1,64,4096]{2,1,0:T(8,128)(2,1)S(1)}, bf16[1,64,4096]{2,1,0:T(8,128)(2,1)S(1)}, u32[]{:S(2)}, u32[]{:S(2)}) %collective-permute-start.2) | collective-permute-done | bytes 524320 | tf_op jit(solution)/shard_map/ppermute | solution.py:26
  28.2 0.0 collective-permute-start.3
  28.2 0.0 collective-permute-done.refs_1_
  28.2 0.0 copy-start
  28.2 12.0 %shard_map.55 = (f32[1,128,4096]{2,1,0:T(8,128)S(1)}, bf16[1,128,4096]{2,1,0:T(8,128)(2,1)S(1)}, bf16[4096,1024]{1,0:T(8,128)(2,1)S(1)}, bf16[4096,512]{1,0:T(8,128)(2,1)S(1)}, bf16[1024,4096]{1,0:T(8,128)(2,1)S(1)}) custom-call(bf16[1,128,4096]{2,1,0:T(8,128)(2,1)} %refs_0_.1, bf16[1,128,4096]{2,1,0:T(8,128)(2,1)S(1)} %collective-permute-done.refs_1_, ...), custom_call_target="tpu_custom_call" | custom-call | flops 5368709120 | bytes 20971520 | tf_op jit(solution)/shard_map/pallas_call | solution.py:226
  40.2 0.0 collective-permute-done.5.refs_1_
  40.2 0.0 copy-done
  40.2 5.7 %shard_map.56 = (f32[1,64,4096]{2,1,0:T(8,128)S(1)}, bf16[1,64,4096]{2,1,0:T(8,128)(2,1)S(1)}, bf16[2,64,512]{2,1,0:T(8,128)(2,1)S(1)}) custom-call(bf16[1,64,4096]{2,1,0:T(8,128)(2,1)S(1)} %collective-permute-done.4.refs_0_, bf16[1,64,4096]{2,1,0:T(8,128)(2,1)S(1)} %collective-permute-done.5.refs_1_, f32[1,4096]{1,0:T(1,128)S(1)} %bitcast.2, ...), custom_call_target="tpu_custom_call" | custom-call | flops 2684354560 | bytes 20971520 | tf_op jit(solution)/shard_map/pallas_call | solution.py:226
  45.9 0.6 collective-permute-start.8
  46.5 0.1 collective-permute-start.1
  46.5 0.0 collective-permute-done.3.refs_1_
  46.5 5.5 %shard_map.57 = (f32[1,64,4096]{2,1,0:T(8,128)S(1)}, bf16[1,64,4096]{2,1,0:T(8,128)(2,1)S(1)}, bf16[2,64,512]{2,1,0:T(8,128)(2,1)}) custom-call(bf16[1,64,4096]{2,1,0:T(8,128)(2,1)S(1)} %collective-permute-done.2.refs_0_, bf16[1,64,4096]{2,1,0:T(8,128)(2,1)S(1)} %collective-permute-done.3.refs_1_, f32[1,4096]{1,0:T(1,128)S(1)} %bitcast.3, ...), custom_call_target="tpu_custom_call" | custom-call | flops 2684354560 | bytes 20971520 | tf_op jit(solution)/shard_map/pallas_call | solution.py:226
  52.0 0.5 collective-permute-start.6
  52.5 0.0 collective-permute-done.8
  52.5 0.1 add_convert_fusion
  52.6 1.8 %collective-permute-start.9 = (bf16[1,64,4096]{2,1,0:T(8,128)(2,1)S(1)}, bf16[1,64,4096]{2,1,0:T(8,128)(2,1)S(1)}, u32[]{:S(2)}, u32[]{:S(2)}) collective-permute-start(bf16[1,64,4096]{2,1,0:T(8,128)(2,1)S(1)} %add_convert_fusion), channel_id=1, source_target_pairs={{0,2},{1,3},{2,0},{3,1},{4,6},{5,7},{6,4},{7,5},{8,10},{9,11},{10,... | collective-permute-start | bytes 1572872 | tf_op jit(solution)/shard_map/ppermute | solution.py:26
  54.4 0.0 collective-permute-done.6
  54.4 0.1 add_convert_fusion.1
  54.5 1.4 %collective-permute-start.7 = (bf16[1,64,4096]{2,1,0:T(8,128)(2,1)S(1)}, bf16[1,64,4096]{2,1,0:T(8,128)(2,1)S(1)}, u32[]{:S(2)}, u32[]{:S(2)}) collective-permute-start(bf16[1,64,4096]{2,1,0:T(8,128)(2,1)S(1)} %add_convert_fusion.1), channel_id=1, source_target_pairs={{0,2},{1,3},{2,0},{3,1},{4,6},{5,7},{6,4},{7,5},{8,10},{9,11},{10,... | collective-permute-start | bytes 1572872 | tf_op jit(solution)/shard_map/ppermute | solution.py:26
  55.9 11.5 %collective-permute-done.9.refs_2_ = bf16[1,64,4096]{2,1,0:T(8,128)(2,1)S(1)} collective-permute-done((bf16[1,64,4096]{2,1,0:T(8,128)(2,1)S(1)}, bf16[1,64,4096]{2,1,0:T(8,128)(2,1)S(1)}, u32[]{:S(2)}, u32[]{:S(2)}) %collective-permute-start.9) | collective-permute-done | bytes 524320 | tf_op jit(solution)/shard_map/ppermute | solution.py:26
  67.5 0.0 collective-permute-done.1.refs_1_
  67.5 1.1 %shard_map.58.refs_3_ = bf16[1,128,4096]{2,1,0:T(8,128)(2,1)} custom-call(f32[1,128,4096]{2,1,0:T(8,128)S(1)} %get-tuple-element.15.refs_0_, bf16[1,128,4096]{2,1,0:T(8,128)(2,1)S(1)} %collective-permute-done.1.refs_1_, bf16[1,64,4096]{2,1,0:T(8,128)(2,1)S(1)} %collective-permute-done.9.refs_2_, bf16[8,128]{1,0:T(8,128)(2,1)S(1)} %broadcast_in_dim.2.refs_3_), custom_call_target="tpu_custom_call" | custom-call | tf_op jit(solution)/shard_map/pallas_call | solution.py:262
  68.5 9.3 %collective-permute-done.7.refs_2_ = bf16[1,64,4096]{2,1,0:T(8,128)(2,1)S(1)} collective-permute-done((bf16[1,64,4096]{2,1,0:T(8,128)(2,1)S(1)}, bf16[1,64,4096]{2,1,0:T(8,128)(2,1)S(1)}, u32[]{:S(2)}, u32[]{:S(2)}) %collective-permute-start.7) | collective-permute-done | bytes 524320 | tf_op jit(solution)/shard_map/ppermute | solution.py:26
  77.8 1.0 %shard_map.59 = bf16[1,128,4096]{2,1,0:T(8,128)(2,1)} custom-call(f32[1,128,4096]{2,1,0:T(8,128)S(1)} %get-tuple-element.15.refs_0_, bf16[1,128,4096]{2,1,0:T(8,128)(2,1)S(1)} %collective-permute-done.1.refs_1_, bf16[1,64,4096]{2,1,0:T(8,128)(2,1)S(1)} %collective-permute-done.7.refs_2_, ...), custom_call_target="tpu_custom_call", output_to_operand_aliasing={{}: (3, {})} | custom-call | tf_op jit(solution)/shard_map/pallas_call | solution.py:262
  (2 shorter events, 0.0 us)
Async XLA Ops:
  0.0 28.2 %collective-permute-start = (bf16[1,128,4096]{2,1,0:T(8,128)(2,1)}, bf16[1,128,4096]{2,1,0:T(8,128)(2,1)S(1)}, u32[]{:S(2)}, u32[]{:S(2)}) collective-permute-start(bf16[1,128,4096]{2,1,0:T(8,128)(2,1)} %refs_0_.1), channel_id=1, source_target_pairs={{0,1},{1,0},{2,3},{3,2},{4,5},{5,4},{6,7},{7,6},{8,9},{9,8},{10,11... | collective-permute-start | bytes 3145736 | tf_op jit(solution)/shard_map/ppermute | solution.py:26
  1.8 15.3 %collective-permute-start.4 = (bf16[1,64,4096]{2,1,0:T(8,128)(2,1)S(1)}, bf16[1,64,4096]{2,1,0:T(8,128)(2,1)S(1)}, u32[]{:S(2)}, u32[]{:S(2)}) collective-permute-start(bf16[1,64,4096]{2,1,0:T(8,128)(2,1)S(1)} %get-tuple-element.25), channel_id=1, source_target_pairs={{0,2},{1,3},{2,0},{3,1},{4,6},{5,7},{6,4},{7,5},{8,10},{9,11},{10,... | collective-permute-start | bytes 1572872 | tf_op jit(solution)/shard_map/ppermute | solution.py:26
  4.3 23.8 %collective-permute-start.2 = (bf16[1,64,4096]{2,1,0:T(8,128)(2,1)S(1)}, bf16[1,64,4096]{2,1,0:T(8,128)(2,1)S(1)}, u32[]{:S(2)}, u32[]{:S(2)}) collective-permute-start(bf16[1,64,4096]{2,1,0:T(8,128)(2,1)S(1)} %get-tuple-element.26), channel_id=1, source_target_pairs={{0,2},{1,3},{2,0},{3,1},{4,6},{5,7},{6,4},{7,5},{8,10},{9,11},{10,... | collective-permute-start | bytes 1572872 | tf_op jit(solution)/shard_map/ppermute | solution.py:26
  17.1 23.1 %collective-permute-start.5 = (bf16[1,64,4096]{2,1,0:T(8,128)(2,1)S(1)}, bf16[1,64,4096]{2,1,0:T(8,128)(2,1)S(1)}, u32[]{:S(2)}, u32[]{:S(2)}) collective-permute-start(bf16[1,64,4096]{2,1,0:T(8,128)(2,1)S(1)} %collective-permute-done.4.refs_0_), channel_id=1, source_target_pairs={{0,1},{1,0},{2,3},{3,2},{4,5},{5,4},{6,7},{7,6},{8,9},{9,8},{10,11... | collective-permute-start | bytes 1572872 | tf_op jit(solution)/shard_map/ppermute | solution.py:26
  28.2 18.4 %collective-permute-start.3 = (bf16[1,64,4096]{2,1,0:T(8,128)(2,1)S(1)}, bf16[1,64,4096]{2,1,0:T(8,128)(2,1)S(1)}, u32[]{:S(2)}, u32[]{:S(2)}) collective-permute-start(bf16[1,64,4096]{2,1,0:T(8,128)(2,1)S(1)} %collective-permute-done.2.refs_0_), channel_id=1, source_target_pairs={{0,1},{1,0},{2,3},{3,2},{4,5},{5,4},{6,7},{7,6},{8,9},{9,8},{10,11... | collective-permute-start | bytes 1572872 | tf_op jit(solution)/shard_map/ppermute | solution.py:26
  28.2 12.0 %copy-start = (f32[4096]{0:T(1024)S(1)}, f32[4096]{0:T(1024)}, u32[]{:S(2)}) copy-start(f32[4096]{0:T(1024)} %param.6) | copy-start | bytes 49156
  45.9 6.6 %collective-permute-start.8 = (bf16[1,64,4096]{2,1,0:T(8,128)(2,1)S(1)}, bf16[1,64,4096]{2,1,0:T(8,128)(2,1)S(1)}, u32[]{:S(2)}, u32[]{:S(2)}) collective-permute-start(bf16[1,64,4096]{2,1,0:T(8,128)(2,1)S(1)} %get-tuple-element.24), channel_id=1, source_target_pairs={{0,1},{1,0},{2,3},{3,2},{4,5},{5,4},{6,7},{7,6},{8,9},{9,8},{10,11... | collective-permute-start | bytes 1572872 | tf_op jit(solution)/shard_map/ppermute | solution.py:26
  46.5 21.0 %collective-permute-start.1 = (bf16[1,128,4096]{2,1,0:T(8,128)(2,1)S(1)}, bf16[1,128,4096]{2,1,0:T(8,128)(2,1)S(1)}, u32[]{:S(2)}, u32[]{:S(2)}) collective-permute-start(bf16[1,128,4096]{2,1,0:T(8,128)(2,1)S(1)} %get-tuple-element.16), channel_id=1, source_target_pairs={{0,1},{1,0},{2,3},{3,2},{4,5},{5,4},{6,7},{7,6},{8,9},{9,8},{10,11... | collective-permute-start | bytes 3145736 | tf_op jit(solution)/shard_map/ppermute | solution.py:26
  52.0 2.4 %collective-permute-start.6 = (bf16[1,64,4096]{2,1,0:T(8,128)(2,1)S(1)}, bf16[1,64,4096]{2,1,0:T(8,128)(2,1)S(1)}, u32[]{:S(2)}, u32[]{:S(2)}) collective-permute-start(bf16[1,64,4096]{2,1,0:T(8,128)(2,1)S(1)} %get-tuple-element.22), channel_id=1, source_target_pairs={{0,1},{1,0},{2,3},{3,2},{4,5},{5,4},{6,7},{7,6},{8,9},{9,8},{10,11... | collective-permute-start | bytes 1572872 | tf_op jit(solution)/shard_map/ppermute | solution.py:26
  52.6 14.9 %collective-permute-start.9 = (bf16[1,64,4096]{2,1,0:T(8,128)(2,1)S(1)}, bf16[1,64,4096]{2,1,0:T(8,128)(2,1)S(1)}, u32[]{:S(2)}, u32[]{:S(2)}) collective-permute-start(bf16[1,64,4096]{2,1,0:T(8,128)(2,1)S(1)} %add_convert_fusion), channel_id=1, source_target_pairs={{0,2},{1,3},{2,0},{3,1},{4,6},{5,7},{6,4},{7,5},{8,10},{9,11},{10,... | collective-permute-start | bytes 1572872 | tf_op jit(solution)/shard_map/ppermute | solution.py:26
  54.5 23.3 %collective-permute-start.7 = (bf16[1,64,4096]{2,1,0:T(8,128)(2,1)S(1)}, bf16[1,64,4096]{2,1,0:T(8,128)(2,1)S(1)}, u32[]{:S(2)}, u32[]{:S(2)}) collective-permute-start(bf16[1,64,4096]{2,1,0:T(8,128)(2,1)S(1)} %add_convert_fusion.1), channel_id=1, source_target_pairs={{0,2},{1,3},{2,0},{3,1},{4,6},{5,7},{6,4},{7,5},{8,10},{9,11},{10,... | collective-permute-start | bytes 1572872 | tf_op jit(solution)/shard_map/ppermute | solution.py:26

commit v3 on v2

--- a/solution.py
+++ b/solution.py
@@ -16,7 +16,7 @@
 THETA = 500000.0
 
 CHUNKS = 2
-K_STEPS = 2
+K_STEPS = 4
 OUT_STEPS = 4
 VMEM_LIMIT = 12 * 2**20
 
@@ -239,37 +239,55 @@
     return result[:pieces], result[pieces:]
 
 
-def finish_kernel(*refs):
-    *addends, _, out = refs
-    total = addends[0][...]
-    for ref in addends[1:]:
-        total = total + ref[...].astype(jnp.float32)
-    out[...] = total.astype(jnp.bfloat16)
+def finish_kernel(*refs, c, near, aliased):
+    own, *addends = refs[: len(refs) - 3 - aliased]
+    out, total_held, sems = refs[-3:]
+    _, chunk, width = total_held.shape
+    span = slice(c * chunk, (c + 1) * chunk)
+    parts = 2
+    copies = []
+    for part in range(parts):
+        columns = slice(part * width // parts, (part + 1) * width // parts)
+        total = own[:, span, columns]
+        for at, ref in enumerate(addends):
+            rows = span if at < near else slice(None)
+            total = total + ref[:, rows, columns].astype(jnp.float32)
+        total_held[:, :, columns] = total.astype(jnp.bfloat16)
+        copies.append(
+            pltpu.make_async_copy(
+                total_held.at[:, :, columns], out.at[:, span, columns], sems.at[part]
+            )
+        )
+        copies[-1].start()
+    for copy in copies:
+        copy.wait()
 
 
 def finish(own, whole_came, came, previous, c, chunk):
     seqs, _, width = own.shape
-    column = width // 2
-    ranged = pl.BlockSpec((seqs, chunk, column), lambda i: (0, c, i))
-    single = pl.BlockSpec((seqs, chunk, column), lambda i: (0, 0, i))
-    addends = [own, *whole_came, *came]
-    specs = [ranged] * (1 + len(whole_came)) + [single] * len(came)
+    vmem = pl.BlockSpec(memory_space=pltpu.VMEM)
+    hbm = pl.BlockSpec(memory_space=pltpu.HBM)
+    operands = [own, *whole_came, *came]
+    specs = [vmem] * len(operands)
     aliases = {}
-    if previous is None:
-        previous = jnp.zeros((8, 128), jnp.bfloat16)
-    else:
-        aliases = {len(addends): 0}
+    if previous is not None:
+        aliases = {len(operands): 0}
+        operands.append(previous)
+        specs.append(hbm)
     return pl.pallas_call(
-        finish_kernel,
-        grid=(width // column,),
-        in_specs=specs + [pl.BlockSpec(memory_space=pl.ANY)],
-        out_specs=ranged,
-        out_shape=jax.ShapeDtypeStruct(own.shape, jnp.bfloat16),
+        functools.partial(
+            finish_kernel, c=c, near=len(whole_came), aliased=int(previous is not None)
+        ),
+        in_specs=specs,
+        out_specs=hbm,
+        out_shape=pltpu.HBM(own.shape, jnp.bfloat16),
+        scratch_shapes=[
+            pltpu.VMEM((seqs, chunk, width), jnp.bfloat16),
+            pltpu.SemaphoreType.DMA((2,)),
+        ],
         input_output_aliases=aliases,
-        compiler_params=pltpu.CompilerParams(
-            dimension_semantics=("arbitrary",), vmem_limit_bytes=16 * 2**20
-        ),
-    )(*addends, previous)
+        compiler_params=pltpu.CompilerParams(vmem_limit_bytes=VMEM_LIMIT),
+    )(*operands)
 
 
 def join_heads(kv_weight):
@@ -304,8 +322,10 @@
     if len(near) > 1:
         arrived[1] = hop(hidden_in, 1)
     far_arrived = []
+    later = hidden_in
     for span in spans:
-        held = {0: hidden_in[:, span]}
+        part, later = lax.optimization_barrier((later[:, span], later))
+        held = {0: part}
         for m in far:
             low = m & -m
             if m ^ low == 1:

time: 79 us -> 81.2 us (1.028)
  Pallas kernels: 25.2 us -> 27.2 us
  waiting for transfers between devices: 44.1 us -> 43.2 us
  local copies, waits for them, and re-layouts: 1.27 us -> 2.15 us
    pallas_call x3, Pallas kernels: 23.1 us -> 25.4 us  [block(): pl.pallas_call(kernel, in_specs=in_specs, out_specs=[vmem] * len(out_shap...]
    ppermute x10, waiting for transfers between devices: 44.1 us -> 43.2 us  [hop(): return lax.ppermute(value, 'tensor', pairs)]
    slice x1 -> x2, local copies, waits for them, and re-layouts: 1.27 us -> 2.15 us  [layer(): part, later = lax.optimization_barrier((later[:, span], later))]
  transfers between devices with their start and end apart: 10 -> 10, of which waited for: 4 -> 4; matrix products, arithmetic and copies ran while one was open for 2% -> 3% of each run, Pallas kernels for 31% -> 32%
where the time goes in v3:
time: 81.2 us; the launch traced here: 81 us
  waiting for transfers between devices  43.2 us (53%)
  Pallas kernels  27.2 us (33%)
  starting transfers between devices  7.54 us (9%)
  local copies, waits for them, and re-layouts  2.15 us (3%)
    ppermute x10, waiting for transfers between devices, hop(): return lax.ppermute(value, 'tensor', pairs)  43.2 us
    pallas_call x3, Pallas kernels, block(): pl.pallas_call(kernel, in_specs=in_specs, out_specs=[vmem] * len(out_shap...  25.4 us
    ppermute x10, starting transfers between devices, hop(): return lax.ppermute(value, 'tensor', pairs)  7.54 us
    slice x2, local copies, waits for them, and re-layouts, layer(): part, later = lax.optimization_barrier((later[:, span], later))  2.15 us
    pallas_call x2, Pallas kernels, finish(): pl.pallas_call(functools.partial(finish_kernel, c=c, near=len(whole_came)...  1.77 us
  transfers between devices with their start and end apart: 10, of which 4 were waited for; matrix products, arithmetic and copies ran while one was open for 3% of the time, Pallas kernels for 32%

profile of v3, /device:TPU:0, one launch (start us, length us, event | category | flops | bytes accessed | tf_op | source)
XLA Modules:
  0.0 81.0 jit_solution(9448432439358772284)
XLA Ops:
  0.0 0.5 collective-permute-start
  0.5 1.1 %slice.18 = bf16[1,64,4096]{2,1,0:T(8,128)(2,1)S(1)} slice(bf16[1,128,4096]{2,1,0:T(8,128)(2,1)} %refs_0_.1), slice={[0:1], [0:64], [0:4096]} | slice | bytes 1048576 | tf_op jit(solution)/shard_map/slice | solution.py:327
  1.6 2.6 %collective-permute-start.4 = (bf16[1,64,4096]{2,1,0:T(8,128)(2,1)S(1)}, bf16[1,64,4096]{2,1,0:T(8,128)(2,1)S(1)}, u32[]{:S(2)}, u32[]{:S(2)}) collective-permute-start(bf16[1,64,4096]{2,1,0:T(8,128)(2,1)S(1)} %slice.18), channel_id=1, source_target_pairs={{0,2},{1,3},{2,0},{3,1},{4,6},{5,7},{6,4},{7,5},{8,10},{9,11},{10,... | collective-permute-start | bytes 1572872 | tf_op jit(solution)/shard_map/ppermute | solution.py:26
  4.1 1.1 %slice.19 = bf16[1,64,4096]{2,1,0:T(8,128)(2,1)S(1)} slice(bf16[1,128,4096]{2,1,0:T(8,128)(2,1)} %refs_0_.1), slice={[0:1], [64:128], [0:4096]} | slice | bytes 1048576 | tf_op jit(solution)/shard_map/slice | solution.py:327
  5.2 0.1 collective-permute-start.2
  5.3 0.3 fusion.6
  5.6 0.1 pad_maximum_fusion
  5.7 11.2 %collective-permute-done.4.refs_0_ = bf16[1,64,4096]{2,1,0:T(8,128)(2,1)S(1)} collective-permute-done((bf16[1,64,4096]{2,1,0:T(8,128)(2,1)S(1)}, bf16[1,64,4096]{2,1,0:T(8,128)(2,1)S(1)}, u32[]{:S(2)}, u32[]{:S(2)}) %collective-permute-start.4) | collective-permute-done | bytes 524320 | tf_op jit(solution)/shard_map/ppermute | solution.py:26
  16.9 0.0 collective-permute-start.5
  16.9 0.1 fusion.3
  17.0 10.9 %collective-permute-done.2.refs_0_ = bf16[1,64,4096]{2,1,0:T(8,128)(2,1)S(1)} collective-permute-done((bf16[1,64,4096]{2,1,0:T(8,128)(2,1)S(1)}, bf16[1,64,4096]{2,1,0:T(8,128)(2,1)S(1)}, u32[]{:S(2)}, u32[]{:S(2)}) %collective-permute-start.2) | collective-permute-done | bytes 524320 | tf_op jit(solution)/shard_map/ppermute | solution.py:26
  28.0 0.0 collective-permute-start.3
  28.0 0.0 collective-permute-done.refs_1_
  28.0 0.0 copy-start
  28.0 14.3 %shard_map.55 = (f32[1,128,4096]{2,1,0:T(8,128)S(1)}, bf16[1,128,4096]{2,1,0:T(8,128)(2,1)S(1)}, bf16[4096,1024]{1,0:T(8,128)(2,1)S(1)}, bf16[4096,512]{1,0:T(8,128)(2,1)S(1)}, bf16[1024,4096]{1,0:T(8,128)(2,1)S(1)}) custom-call(bf16[1,128,4096]{2,1,0:T(8,128)(2,1)} %refs_0_.1, bf16[1,128,4096]{2,1,0:T(8,128)(2,1)S(1)} %collective-permute-done.refs_1_, ...), custom_call_target="tpu_custom_call" | custom-call | flops 5368709120 | bytes 20971520 | tf_op jit(solution)/shard_map/pallas_call | solution.py:226
  42.3 0.0 collective-permute-done.5.refs_1_
  42.3 0.0 copy-done
  42.4 5.6 %shard_map.56 = (f32[1,64,4096]{2,1,0:T(8,128)S(1)}, bf16[1,64,4096]{2,1,0:T(8,128)(2,1)S(1)}, bf16[2,64,512]{2,1,0:T(8,128)(2,1)S(1)}) custom-call(bf16[1,64,4096]{2,1,0:T(8,128)(2,1)S(1)} %collective-permute-done.4.refs_0_, bf16[1,64,4096]{2,1,0:T(8,128)(2,1)S(1)} %collective-permute-done.5.refs_1_, f32[1,4096]{1,0:T(1,128)S(1)} %bitcast.2, ...), custom_call_target="tpu_custom_call" | custom-call | flops 2684354560 | bytes 20971520 | tf_op jit(solution)/shard_map/pallas_call | solution.py:226
  48.0 0.6 collective-permute-start.8
  48.6 0.1 collective-permute-start.1
  48.6 0.0 collective-permute-done.3.refs_1_
  48.6 5.5 %shard_map.57 = (f32[1,64,4096]{2,1,0:T(8,128)S(1)}, bf16[1,64,4096]{2,1,0:T(8,128)(2,1)S(1)}, bf16[2,64,512]{2,1,0:T(8,128)(2,1)}) custom-call(bf16[1,64,4096]{2,1,0:T(8,128)(2,1)S(1)} %collective-permute-done.2.refs_0_, bf16[1,64,4096]{2,1,0:T(8,128)(2,1)S(1)} %collective-permute-done.3.refs_1_, f32[1,4096]{1,0:T(1,128)S(1)} %bitcast.3, ...), custom_call_target="tpu_custom_call" | custom-call | flops 2684354560 | bytes 20971520 | tf_op jit(solution)/shard_map/pallas_call | solution.py:226
  54.1 0.5 collective-permute-start.6
  54.6 0.0 collective-permute-done.8
  54.6 0.1 add_convert_fusion
  54.7 1.8 %collective-permute-start.9 = (bf16[1,64,4096]{2,1,0:T(8,128)(2,1)S(1)}, bf16[1,64,4096]{2,1,0:T(8,128)(2,1)S(1)}, u32[]{:S(2)}, u32[]{:S(2)}) collective-permute-start(bf16[1,64,4096]{2,1,0:T(8,128)(2,1)S(1)} %add_convert_fusion), channel_id=1, source_target_pairs={{0,2},{1,3},{2,0},{3,1},{4,6},{5,7},{6,4},{7,5},{8,10},{9,11},{10,... | collective-permute-start | bytes 1572872 | tf_op jit(solution)/shard_map/ppermute | solution.py:26
  56.5 0.0 collective-permute-done.6
  56.5 0.1 add_convert_fusion.1
  56.6 1.4 %collective-permute-start.7 = (bf16[1,64,4096]{2,1,0:T(8,128)(2,1)S(1)}, bf16[1,64,4096]{2,1,0:T(8,128)(2,1)S(1)}, u32[]{:S(2)}, u32[]{:S(2)}) collective-permute-start(bf16[1,64,4096]{2,1,0:T(8,128)(2,1)S(1)} %add_convert_fusion.1), channel_id=1, source_target_pairs={{0,2},{1,3},{2,0},{3,1},{4,6},{5,7},{6,4},{7,5},{8,10},{9,11},{10,... | collective-permute-start | bytes 1572872 | tf_op jit(solution)/shard_map/ppermute | solution.py:26
  58.1 11.5 %collective-permute-done.9.refs_2_ = bf16[1,64,4096]{2,1,0:T(8,128)(2,1)S(1)} collective-permute-done((bf16[1,64,4096]{2,1,0:T(8,128)(2,1)S(1)}, bf16[1,64,4096]{2,1,0:T(8,128)(2,1)S(1)}, u32[]{:S(2)}, u32[]{:S(2)}) %collective-permute-start.9) | collective-permute-done | bytes 524320 | tf_op jit(solution)/shard_map/ppermute | solution.py:26
  69.6 0.0 collective-permute-done.1.refs_1_
  69.6 0.9 %shard_map.58.refs_3_ = bf16[1,128,4096]{2,1,0:T(8,128)(2,1)} custom-call(f32[1,128,4096]{2,1,0:T(8,128)S(1)} %get-tuple-element.18.refs_0_, bf16[1,128,4096]{2,1,0:T(8,128)(2,1)S(1)} %collective-permute-done.1.refs_1_, bf16[1,64,4096]{2,1,0:T(8,128)(2,1)S(1)} %collective-permute-done.9.refs_2_), custom_call_target="tpu_custom_call" | custom-call | tf_op jit(solution)/shard_map/pallas_call | solution.py:277
  70.5 9.4 %collective-permute-done.7.refs_2_ = bf16[1,64,4096]{2,1,0:T(8,128)(2,1)S(1)} collective-permute-done((bf16[1,64,4096]{2,1,0:T(8,128)(2,1)S(1)}, bf16[1,64,4096]{2,1,0:T(8,128)(2,1)S(1)}, u32[]{:S(2)}, u32[]{:S(2)}) %collective-permute-start.7) | collective-permute-done | bytes 524320 | tf_op jit(solution)/shard_map/ppermute | solution.py:26
  79.9 0.9 %shard_map.59 = bf16[1,128,4096]{2,1,0:T(8,128)(2,1)} custom-call(f32[1,128,4096]{2,1,0:T(8,128)S(1)} %get-tuple-element.18.refs_0_, bf16[1,128,4096]{2,1,0:T(8,128)(2,1)S(1)} %collective-permute-done.1.refs_1_, bf16[1,64,4096]{2,1,0:T(8,128)(2,1)S(1)} %collective-permute-done.7.refs_2_, ...), custom_call_target="tpu_custom_call", output_to_operand_aliasing={{}: (3, {})} | custom-call | tf_op jit(solution)/shard_map/pallas_call | solution.py:277
  (1 shorter events, 0.0 us)
Async XLA Ops:
  0.0 28.0 %collective-permute-start = (bf16[1,128,4096]{2,1,0:T(8,128)(2,1)}, bf16[1,128,4096]{2,1,0:T(8,128)(2,1)S(1)}, u32[]{:S(2)}, u32[]{:S(2)}) collective-permute-start(bf16[1,128,4096]{2,1,0:T(8,128)(2,1)} %refs_0_.1), channel_id=1, source_target_pairs={{0,1},{1,0},{2,3},{3,2},{4,5},{5,4},{6,7},{7,6},{8,9},{9,8},{10,11... | collective-permute-start | bytes 3145736 | tf_op jit(solution)/shard_map/ppermute | solution.py:26
  1.6 15.3 %collective-permute-start.4 = (bf16[1,64,4096]{2,1,0:T(8,128)(2,1)S(1)}, bf16[1,64,4096]{2,1,0:T(8,128)(2,1)S(1)}, u32[]{:S(2)}, u32[]{:S(2)}) collective-permute-start(bf16[1,64,4096]{2,1,0:T(8,128)(2,1)S(1)} %slice.18), channel_id=1, source_target_pairs={{0,2},{1,3},{2,0},{3,1},{4,6},{5,7},{6,4},{7,5},{8,10},{9,11},{10,... | collective-permute-start | bytes 1572872 | tf_op jit(solution)/shard_map/ppermute | solution.py:26
  5.2 22.8 %collective-permute-start.2 = (bf16[1,64,4096]{2,1,0:T(8,128)(2,1)S(1)}, bf16[1,64,4096]{2,1,0:T(8,128)(2,1)S(1)}, u32[]{:S(2)}, u32[]{:S(2)}) collective-permute-start(bf16[1,64,4096]{2,1,0:T(8,128)(2,1)S(1)} %slice.19), channel_id=1, source_target_pairs={{0,2},{1,3},{2,0},{3,1},{4,6},{5,7},{6,4},{7,5},{8,10},{9,11},{10,... | collective-permute-start | bytes 1572872 | tf_op jit(solution)/shard_map/ppermute | solution.py:26
  16.9 25.4 %collective-permute-start.5 = (bf16[1,64,4096]{2,1,0:T(8,128)(2,1)S(1)}, bf16[1,64,4096]{2,1,0:T(8,128)(2,1)S(1)}, u32[]{:S(2)}, u32[]{:S(2)}) collective-permute-start(bf16[1,64,4096]{2,1,0:T(8,128)(2,1)S(1)} %collective-permute-done.4.refs_0_), channel_id=1, source_target_pairs={{0,1},{1,0},{2,3},{3,2},{4,5},{5,4},{6,7},{7,6},{8,9},{9,8},{10,11... | collective-permute-start | bytes 1572872 | tf_op jit(solution)/shard_map/ppermute | solution.py:26
  28.0 20.7 %collective-permute-start.3 = (bf16[1,64,4096]{2,1,0:T(8,128)(2,1)S(1)}, bf16[1,64,4096]{2,1,0:T(8,128)(2,1)S(1)}, u32[]{:S(2)}, u32[]{:S(2)}) collective-permute-start(bf16[1,64,4096]{2,1,0:T(8,128)(2,1)S(1)} %collective-permute-done.2.refs_0_), channel_id=1, source_target_pairs={{0,1},{1,0},{2,3},{3,2},{4,5},{5,4},{6,7},{7,6},{8,9},{9,8},{10,11... | collective-permute-start | bytes 1572872 | tf_op jit(solution)/shard_map/ppermute | solution.py:26
  28.0 14.4 %copy-start = (f32[4096]{0:T(1024)S(1)}, f32[4096]{0:T(1024)}, u32[]{:S(2)}) copy-start(f32[4096]{0:T(1024)} %param.6) | copy-start | bytes 49156
  48.0 6.6 %collective-permute-start.8 = (bf16[1,64,4096]{2,1,0:T(8,128)(2,1)S(1)}, bf16[1,64,4096]{2,1,0:T(8,128)(2,1)S(1)}, u32[]{:S(2)}, u32[]{:S(2)}) collective-permute-start(bf16[1,64,4096]{2,1,0:T(8,128)(2,1)S(1)} %get-tuple-element.30), channel_id=1, source_target_pairs={{0,1},{1,0},{2,3},{3,2},{4,5},{5,4},{6,7},{7,6},{8,9},{9,8},{10,11... | collective-permute-start | bytes 1572872 | tf_op jit(solution)/shard_map/ppermute | solution.py:26
  48.6 21.0 %collective-permute-start.1 = (bf16[1,128,4096]{2,1,0:T(8,128)(2,1)S(1)}, bf16[1,128,4096]{2,1,0:T(8,128)(2,1)S(1)}, u32[]{:S(2)}, u32[]{:S(2)}) collective-permute-start(bf16[1,128,4096]{2,1,0:T(8,128)(2,1)S(1)} %get-tuple-element.19), channel_id=1, source_target_pairs={{0,1},{1,0},{2,3},{3,2},{4,5},{5,4},{6,7},{7,6},{8,9},{9,8},{10,11... | collective-permute-start | bytes 3145736 | tf_op jit(solution)/shard_map/ppermute | solution.py:26
  54.1 2.4 %collective-permute-start.6 = (bf16[1,64,4096]{2,1,0:T(8,128)(2,1)S(1)}, bf16[1,64,4096]{2,1,0:T(8,128)(2,1)S(1)}, u32[]{:S(2)}, u32[]{:S(2)}) collective-permute-start(bf16[1,64,4096]{2,1,0:T(8,128)(2,1)S(1)} %get-tuple-element.28), channel_id=1, source_target_pairs={{0,1},{1,0},{2,3},{3,2},{4,5},{5,4},{6,7},{7,6},{8,9},{9,8},{10,11... | collective-permute-start | bytes 1572872 | tf_op jit(solution)/shard_map/ppermute | solution.py:26
  54.7 14.9 %collective-permute-start.9 = (bf16[1,64,4096]{2,1,0:T(8,128)(2,1)S(1)}, bf16[1,64,4096]{2,1,0:T(8,128)(2,1)S(1)}, u32[]{:S(2)}, u32[]{:S(2)}) collective-permute-start(bf16[1,64,4096]{2,1,0:T(8,128)(2,1)S(1)} %add_convert_fusion), channel_id=1, source_target_pairs={{0,2},{1,3},{2,0},{3,1},{4,6},{5,7},{6,4},{7,5},{8,10},{9,11},{10,... | collective-permute-start | bytes 1572872 | tf_op jit(solution)/shard_map/ppermute | solution.py:26
  56.6 23.3 %collective-permute-start.7 = (bf16[1,64,4096]{2,1,0:T(8,128)(2,1)S(1)}, bf16[1,64,4096]{2,1,0:T(8,128)(2,1)S(1)}, u32[]{:S(2)}, u32[]{:S(2)}) collective-permute-start(bf16[1,64,4096]{2,1,0:T(8,128)(2,1)S(1)} %add_convert_fusion.1), channel_id=1, source_target_pairs={{0,2},{1,3},{2,0},{3,1},{4,6},{5,7},{6,4},{7,5},{8,10},{9,11},{10,... | collective-permute-start | bytes 1572872 | tf_op jit(solution)/shard_map/ppermute | solution.py:26
